TPU v7x, 256 devices: a whole 4x4x8 slice. The times are simulated.
256 devices in a mesh: gx: 4 (over x), gy: 8 (over y, core), gz: 8 (over z).
Axes of the slice: x: 4, y: 4, z: 8, core: 2. Of those that a mesh axis runs over, the one named last changes fastest.
Arguments:
- right_side: float32 [8, 32, 256, 1024], P(None, 'gx', 'gy', 'gz'), may hold values from -12 to 12
- shift: float32 [32, 256, 1024], P('gx', 'gy', 'gz'), may hold values from 0.02 to 2
Outputs:
- solution_block: float32 [8, 32, 256, 1024], P(None, 'gx', 'gy', 'gz')
- residual_norms: float32 [8], replicated
All inputs are finite; a program needn't handle non-finite values.
Results may differ from a plain program's by a relative error of at most 0.0003.
Values sent between devices are 32-bit elements; how exact they have to be, the bound alone decides.
A program may use at most 128 MiB of HBM per device.

v0:
```python
import jax
import jax.numpy as jnp
from jax import lax
from jax.sharding import Mesh
from jax.sharding import PartitionSpec as P

ITERS = 2
GX_GY_GZ = ("gx", "gy_0", "gy_1", "gz")
GY = ("gy_0", "gy_1")


def padded_2(value, sides, width):
    edges = {}
    for axis, dim in sides:
        devices, length = (lax.axis_size(axis), value.shape[dim])
        up = [(i, (i + 1) % devices) for i in range(devices - 1)]
        last = lax.slice_in_dim(value, length - width, length, axis=dim)
        leading = lax.slice_in_dim(value, 0, width, axis=dim)
        edges[dim] = (
            lax.ppermute(last, axis, up),
            lax.ppermute(leading, axis, [(b, a) for a, b in up]),
        )
    done = []
    for _, dim in sides:
        low, high = edges[dim]
        around = [(width, width) if d in done else (0, 0) for d in range(value.ndim)]
        value = jnp.concatenate([jnp.pad(low, around), value, jnp.pad(high, around)], axis=dim)
        done.append(dim)
    return value


def by_axis(value, axes):
    for axis in axes:
        value = lax.psum(value, axis)
    return value


def operate(fields, shift):
    padded = padded_2(fields, (("gx", 1), (GY, 2), ("gz", 3)), 1)
    beside = padded[:, 2:, 1:-1, 1:-1] + padded[:, :-2, 1:-1, 1:-1]
    beside = beside + padded[:, 1:-1, 2:, 1:-1] + padded[:, 1:-1, :-2, 1:-1]
    beside = beside + padded[:, 1:-1, 1:-1, 2:] + padded[:, 1:-1, 1:-1, :-2]
    return (6.0 + shift)[None] * fields - beside


def lower_inverse(lower):
    count = lower.shape[0]
    return jax.scipy.linalg.solve_triangular(lower, jnp.eye(count, dtype=lower.dtype), lower=True)


def small_dot(left, right):
    return jnp.dot(left, right, precision=lax.Precision.HIGHEST)


def body(right_side, shift):
    width = right_side.shape[0]
    shape = right_side.shape
    rows = right_side.reshape(width, -1)
    first_step = None
    images = operate(right_side, shift).reshape(width, -1)
    both = jnp.concatenate([rows, images], axis=0)
    joint = by_axis(small_dot(both, both.T), GX_GY_GZ)
    lower = jnp.linalg.cholesky(joint[:width, :width])
    start_coeff = lower.T
    inverse = lower_inverse(lower)
    first_basis = small_dot(inverse, rows)
    basis = [first_basis]
    first_image = small_dot(inverse, images)
    first_coeffs = small_dot(small_dot(inverse, joint[:width, width:]), inverse.T)
    first_self = small_dot(small_dot(inverse, joint[width:, width:]), inverse.T)
    first_gram = first_self - small_dot(first_coeffs.T, first_coeffs)
    first_projected = first_image - small_dot(first_coeffs.T, first_basis)
    first_step = (first_coeffs, first_gram, first_projected)
    hessen = jnp.zeros(((ITERS + 1) * width, ITERS * width), jnp.float32)
    for step in range(ITERS):
        if step == 0 and first_step is not None:
            coeffs, gram, projected = first_step
        else:
            image = operate(basis[step].reshape(shape), shift).reshape(width, -1)
            stacked = jnp.concatenate(basis, axis=0)
            products = by_axis(
                small_dot(jnp.concatenate([stacked, image], axis=0), image.T), GX_GY_GZ
            )
            coeffs = products[:-width]
            gram = products[-width:] - small_dot(coeffs.T, coeffs)
            projected = image - small_dot(coeffs.T, stacked)
        lower = jnp.linalg.cholesky(gram)
        hessen = hessen.at[: (step + 1) * width, step * width : (step + 1) * width].set(coeffs)
        hessen = hessen.at[
            (step + 1) * width : (step + 2) * width, step * width : (step + 1) * width
        ].set(lower.T)
        if step + 1 < ITERS:
            basis.append(small_dot(lower_inverse(lower), projected))
    target = jnp.zeros(((ITERS + 1) * width, width), jnp.float32).at[:width].set(start_coeff)
    normal = small_dot(hessen.T, hessen)
    factor = jnp.linalg.cholesky(normal)
    coeff_y = jax.scipy.linalg.cho_solve((factor, True), small_dot(hessen.T, target))
    solution = small_dot(coeff_y.T, jnp.concatenate(basis, axis=0)).reshape(shape)
    leftover = target - small_dot(hessen, coeff_y)
    norms = jnp.sqrt(jnp.sum(leftover * leftover, axis=0))
    return (solution, norms)


def solution(mesh):
    split = Mesh(
        mesh.devices.reshape(mesh.shape["gx"], 4, 2, mesh.shape["gz"]), ("gx", "gy_0", "gy_1", "gz")
    )
    return jax.shard_map(
        body,
        mesh=split,
        in_specs=(P(None, "gx", GY, "gz"), P("gx", GY, "gz")),
        out_specs=(P(None, "gx", GY, "gz"), P()),
        check_vma=False,
    )
```

profile of v0, /device:TPU:8, one launch (start us, length us, event | category | flops | bytes accessed | tf_op | source)
XLA Modules:
  0.0 174.2 jit_solution(10873587700840309843)
XLA Ops:
  0.6 1.7 fusion.68
  2.3 3.4 %collective-permute-start.1 = (f32[8,1,32,128]{3,2,1,0:T(8,128)}, f32[8,1,32,128]{3,2,1,0:T(8,128)S(1)}, u32[]{:S(2)}, u32[]{:S(2)}) collective-permute-start(f32[8,1,32,128]{3,2,1,0:T(8,128)} %get-tuple-element.79), channel_id=1, source_target_pairs={{0,64},{64,128},{128,192},{1,65},{65,129},{129,193},{2,66},{66,130... | collective-permute-start | bytes 393224 | tf_op jit(solution)/shard_map/ppermute | solution.py:20
  5.7 1.9 %fusion.66 = (f32[8,8,32,1]{3,2,1,0:T(8,128)S(1)}, f32[8,8,32,1]{3,2,1,0:T(8,128)S(1)}) fusion(f32[8,8,32,128]{3,2,1,0:T(8,128)} %param.15), kind=kLoop, calls=%fused_computation.126 | loop fusion | bytes 32768 | tf_op jit(solution)/shard_map/slice | solution.py:18
  7.7 1.0 copy.56
  8.7 1.3 collective-permute-start.4
  10.0 1.0 copy.57
  11.0 4.7 %collective-permute-start.5 = (f32[8,8,32,1]{2,1,3,0:T(8,128)}, f32[8,8,32,1]{2,1,3,0:T(8,128)S(1)}, u32[]{:S(2)}, u32[]{:S(2)}) collective-permute-start(f32[8,8,32,1]{2,1,3,0:T(8,128)} %copy.57), channel_id=1, source_target_pairs={{0,1},{1,2},{2,3},{3,4},{4,5},{5,6},{6,7},{8,9},{9,10},{10,11},{11... | collective-permute-start | bytes 24584 | tf_op jit(solution)/shard_map/ppermute | solution.py:20
  15.8 1.9 %collective-permute-start.2 = (f32[8,8,1,128]{3,2,1,0:T(1,128)S(1)}, f32[8,8,1,128]{3,2,1,0:T(1,128)S(1)}, u32[]{:S(2)}, u32[]{:S(2)}) collective-permute-start(f32[8,8,1,128]{3,2,1,0:T(1,128)S(1)} %get-tuple-element.77), channel_id=1, source_target_pairs={{8,0},{16,8},{24,16},{32,24},{40,32},{48,40},{56,48},{9,1},{17,9},... | collective-permute-start | bytes 98312 | tf_op jit(solution)/shard_map/ppermute | solution.py:21
  17.7 2.4 %collective-permute-start.3 = (f32[8,8,1,128]{3,2,1,0:T(1,128)S(1)}, f32[8,8,1,128]{3,2,1,0:T(1,128)S(1)}, u32[]{:S(2)}, u32[]{:S(2)}) collective-permute-start(f32[8,8,1,128]{3,2,1,0:T(1,128)S(1)} %get-tuple-element.76), channel_id=1, source_target_pairs={{0,8},{8,16},{16,24},{24,32},{32,40},{40,48},{48,56},{1,9},{9,17},... | collective-permute-start | bytes 98312 | tf_op jit(solution)/shard_map/ppermute | solution.py:20
  20.8 1.3 collective-permute-start
  22.1 2.2 %copy.60 = f32[8,8,32,1]{3,2,1,0:T(8,128)} copy(f32[8,8,32,1]{2,1,3,0:T(8,128)} %collective-permute-done.4) | data formatting | bytes 16384
  24.3 1.4 copy.61
  25.9 2.9 %collective-permute-done = f32[8,1,32,128]{3,2,1,0:T(8,128)S(1)} collective-permute-done((f32[8,1,32,128]{3,2,1,0:T(8,128)S(1)}, f32[8,1,32,128]{3,2,1,0:T(8,128)S(1)}, u32[]{:S(2)}, u32[]{:S(2)}) %collective-permute-start) | collective-permute-done | bytes 131104 | tf_op jit(solution)/shard_map/ppermute | solution.py:21
  28.9 1.2 fusion.26
  30.7 2.9 %fusion.6 = f32[16,16]{0,1:T(8,128)S(1)} fusion(f32[8,32768]{1,0:T(8,128)S(1)} %bitcast.94, f32[8,32768]{1,0:T(8,128)S(1)} %bitcast.92), kind=kOutput, calls=%fused_computation.7 | convolution fusion | flops 101187584 | bytes 2098176 | tf_op jit(solution)/shard_map/dot_general | solution.py:52
  33.5 10.3 %psum.56 = f32[16,16]{0,1:T(8,128)S(1)} all-reduce(f32[16,16]{0,1:T(8,128)S(1)} %fusion.6), channel_id=1, replica_groups=mesh['gx'=4,'gy_0'=4,'gy_1'=2,'gz'=8] {'gx'}, use_global_device_ids=true, to_apply=%region_0.1 | all-reduce | flops 256 | bytes 2048 | tf_op jit(solution)/shard_map/psum | solution.py:34
  43.8 8.8 %psum.57 = f32[16,16]{0,1:T(8,128)S(1)} all-reduce(f32[16,16]{0,1:T(8,128)S(1)} %psum.56), channel_id=1, replica_groups=mesh['gx'=4,'gy_0'=4,'gy_1'=2,'gz'=8] {'gy_0'}, use_global_device_ids=true, to_apply=%region_1.2 | all-reduce | flops 256 | bytes 2048 | tf_op jit(solution)/shard_map/psum | solution.py:34
  52.6 2.5 %psum.58 = f32[16,16]{0,1:T(8,128)S(1)} all-reduce(f32[16,16]{0,1:T(8,128)S(1)} %psum.57), channel_id=1, replica_groups=mesh['gx'=4,'gy_0'=4,'gy_1'=2,'gz'=8] {'gy_1'}, use_global_device_ids=true, to_apply=%region_2.3 | all-reduce | flops 256 | bytes 2048 | tf_op jit(solution)/shard_map/psum | solution.py:34
  55.1 19.4 %psum.59 = f32[16,16]{0,1:T(8,128)S(1)} all-reduce(f32[16,16]{0,1:T(8,128)S(1)} %psum.58), channel_id=1, replica_groups=mesh['gx'=4,'gy_0'=4,'gy_1'=2,'gz'=8] {'gz'}, use_global_device_ids=true, to_apply=%region_3.4 | all-reduce | flops 256 | bytes 2048 | tf_op jit(solution)/shard_map/psum | solution.py:34
  77.6 1.5 fusion.62
  79.1 1.5 fusion.61
  84.2 1.0 convolution_subtract_fusion
  85.2 1.0 fusion.72
  86.3 1.7 fusion.63
  88.8 1.7 collective-permute-start.7
  91.2 1.7 copy.58
  92.8 1.3 collective-permute-start.10
  94.1 2.3 %copy.59 = f32[8,8,32,1]{2,1,3,0:T(8,128)} copy(f32[8,8,32,1]{3,0,2,1:T(8,128)} %get-tuple-element.69) | data formatting | bytes 16384
  96.4 5.1 %collective-permute-start.11 = (f32[8,8,32,1]{2,1,3,0:T(8,128)}, f32[8,8,32,1]{2,1,3,0:T(8,128)}, u32[]{:S(2)}, u32[]{:S(2)}) collective-permute-start(f32[8,8,32,1]{2,1,3,0:T(8,128)} %copy.59), channel_id=1, source_target_pairs={{0,1},{1,2},{2,3},{3,4},{4,5},{5,6},{6,7},{8,9},{9,10},{10,11},{11... | collective-permute-start | bytes 24584 | tf_op jit(solution)/shard_map/ppermute | solution.py:20
  101.5 1.9 %collective-permute-start.8 = (f32[8,8,1,128]{3,2,1,0:T(1,128)}, f32[8,8,1,128]{3,2,1,0:T(1,128)}, u32[]{:S(2)}, u32[]{:S(2)}) collective-permute-start(f32[8,8,1,128]{3,2,1,0:T(1,128)} %get-tuple-element.71), channel_id=1, source_target_pairs={{8,0},{16,8},{24,16},{32,24},{40,32},{48,40},{56,48},{9,1},{17,9},... | collective-permute-start | bytes 98312 | tf_op jit(solution)/shard_map/ppermute | solution.py:21
  103.5 2.4 %collective-permute-start.9 = (f32[8,8,1,128]{3,2,1,0:T(1,128)}, f32[8,8,1,128]{3,2,1,0:T(1,128)}, u32[]{:S(2)}, u32[]{:S(2)}) collective-permute-start(f32[8,8,1,128]{3,2,1,0:T(1,128)} %get-tuple-element.70), channel_id=1, source_target_pairs={{0,8},{8,16},{16,24},{24,32},{32,40},{40,48},{48,56},{1,9},{9,17},... | collective-permute-start | bytes 98312 | tf_op jit(solution)/shard_map/ppermute | solution.py:20
  107.6 1.5 collective-permute-start.6
  109.1 2.2 %copy.62 = f32[8,8,32,1]{3,2,1,0:T(8,128)} copy(f32[8,8,32,1]{2,1,3,0:T(8,128)} %collective-permute-done.10) | data formatting | bytes 16384
  111.3 2.2 %copy.63 = f32[8,8,32,1]{3,2,1,0:T(8,128)} copy(f32[8,8,32,1]{2,1,3,0:T(8,128)} %collective-permute-done.11) | data formatting | bytes 16384
  113.5 0.8 pad.51
  114.3 0.8 pad.52
  116.6 1.2 fusion.18
  118.4 3.0 %fusion = f32[24,8]{0,1:T(8,128)S(1)} fusion(f32[8,32768]{1,0:T(8,128)S(1)} %bitcast.96, f32[8,32768]{1,0:T(8,128)S(1)} %fusion.72, f32[8,32768]{1,0:T(8,128)S(1)} %fusion.61), kind=kOutput, calls=%fused_computation.1 | convolution fusion | flops 77070336 | bytes 3146496 | tf_op jit(solution)/shard_map/dot_general | solution.py:52
  121.4 10.4 %psum.60 = f32[24,8]{0,1:T(8,128)S(1)} all-reduce(f32[24,8]{0,1:T(8,128)S(1)} %fusion), channel_id=1, replica_groups=mesh['gx'=4,'gy_0'=4,'gy_1'=2,'gz'=8] {'gx'}, use_global_device_ids=true, to_apply=%region_7.10 | all-reduce | flops 192 | bytes 1536 | tf_op jit(solution)/shard_map/psum | solution.py:34
  131.8 10.7 %psum.61 = f32[24,8]{0,1:T(8,128)S(1)} all-reduce(f32[24,8]{0,1:T(8,128)S(1)} %psum.60), channel_id=1, replica_groups=mesh['gx'=4,'gy_0'=4,'gy_1'=2,'gz'=8] {'gy_0'}, use_global_device_ids=true, to_apply=%region_8.11 | all-reduce | flops 192 | bytes 1536 | tf_op jit(solution)/shard_map/psum | solution.py:34
  142.5 2.5 %psum.62 = f32[24,8]{0,1:T(8,128)S(1)} all-reduce(f32[24,8]{0,1:T(8,128)S(1)} %psum.61), channel_id=1, replica_groups=mesh['gx'=4,'gy_0'=4,'gy_1'=2,'gz'=8] {'gy_1'}, use_global_device_ids=true, to_apply=%region_9.12 | all-reduce | flops 192 | bytes 1536 | tf_op jit(solution)/shard_map/psum | solution.py:34
  144.9 15.0 %psum.63 = f32[24,8]{0,1:T(8,128)S(1)} all-reduce(f32[24,8]{0,1:T(8,128)S(1)} %psum.62), channel_id=1, replica_groups=mesh['gx'=4,'gy_0'=4,'gy_1'=2,'gz'=8] {'gz'}, use_global_device_ids=true, to_apply=%region_10.13 | all-reduce | flops 192 | bytes 1536 | tf_op jit(solution)/shard_map/psum | solution.py:34
  162.2 2.0 %dynamic-slice_select_fusion = f32[16,8]{0,1:T(8,128)S(1)} fusion(f32[24,16]{0,1:T(8,128)S(1)} %scatter.19, s32[]{:T(128)} %bitcast.8, s32[]{:T(128)} %bitcast.9, f32[24,8]{0,1:T(8,128)S(1)} %psum.63, pred[]{:T(512)} %and_reduce_fusion), kind=kLoop, calls=%fused_computation.105 | loop fusion | flops 128 | bytes 1545 | tf_op jit(solution)/shard_map/select.25
  164.1 1.7 scatter.20
  166.6 1.5 cholesky.41
  169.4 1.2 custom-call.15
  171.4 1.1 fusion.10
  173.0 1.2 copy.51
  (87 shorter events, 19.2 us)
Async XLA Ops:
  2.3 23.5 %collective-permute-start.1 = (f32[8,1,32,128]{3,2,1,0:T(8,128)}, f32[8,1,32,128]{3,2,1,0:T(8,128)S(1)}, u32[]{:S(2)}, u32[]{:S(2)}) collective-permute-start(f32[8,1,32,128]{3,2,1,0:T(8,128)} %get-tuple-element.79), channel_id=1, source_target_pairs={{0,64},{64,128},{128,192},{1,65},{65,129},{129,193},{2,66},{66,130... | collective-permute-start | bytes 393224 | tf_op jit(solution)/shard_map/ppermute | solution.py:20
  7.6 8.1 %copy-start = (f32[8,8,32,128]{3,2,1,0:T(8,128)S(1)}, f32[8,8,32,128]{3,2,1,0:T(8,128)}, u32[]{:S(2)}) copy-start(f32[8,8,32,128]{3,2,1,0:T(8,128)} %param.15) | copy-start | bytes 3145732
  7.6 12.5 %copy-start.5 = (f32[8,32,128]{2,1,0:T(8,128)S(1)}, f32[8,32,128]{2,1,0:T(8,128)}, u32[]{:S(2)}) copy-start(f32[8,32,128]{2,1,0:T(8,128)} %param.16) | copy-start | bytes 393220
  8.7 12.1 %collective-permute-start.4 = (f32[8,8,32,1]{2,1,3,0:T(8,128)}, f32[8,8,32,1]{2,1,3,0:T(8,128)}, u32[]{:S(2)}, u32[]{:S(2)}) collective-permute-start(f32[8,8,32,1]{2,1,3,0:T(8,128)} %copy.56), channel_id=1, source_target_pairs={{1,0},{2,1},{3,2},{4,3},{5,4},{6,5},{7,6},{9,8},{10,9},{11,10},{12... | collective-permute-start | bytes 24584 | tf_op jit(solution)/shard_map/ppermute | solution.py:21
  11.0 9.8 %copy-start.6 = (f32[8,1,32,128]{3,2,1,0:T(8,128)S(1)}, f32[8,1,32,128]{3,2,1,0:T(8,128)}, u32[]{:S(2)}) copy-start(f32[8,1,32,128]{3,2,1,0:T(8,128)} %get-tuple-element.78) | copy-start | bytes 393220
  11.0 13.3 %collective-permute-start.5 = (f32[8,8,32,1]{2,1,3,0:T(8,128)}, f32[8,8,32,1]{2,1,3,0:T(8,128)S(1)}, u32[]{:S(2)}, u32[]{:S(2)}) collective-permute-start(f32[8,8,32,1]{2,1,3,0:T(8,128)} %copy.57), channel_id=1, source_target_pairs={{0,1},{1,2},{2,3},{3,4},{4,5},{5,6},{6,7},{8,9},{9,10},{10,11},{11... | collective-permute-start | bytes 24584 | tf_op jit(solution)/shard_map/ppermute | solution.py:20
  15.8 10.0 %collective-permute-start.2 = (f32[8,8,1,128]{3,2,1,0:T(1,128)S(1)}, f32[8,8,1,128]{3,2,1,0:T(1,128)S(1)}, u32[]{:S(2)}, u32[]{:S(2)}) collective-permute-start(f32[8,8,1,128]{3,2,1,0:T(1,128)S(1)} %get-tuple-element.77), channel_id=1, source_target_pairs={{8,0},{16,8},{24,16},{32,24},{40,32},{48,40},{56,48},{9,1},{17,9},... | collective-permute-start | bytes 98312 | tf_op jit(solution)/shard_map/ppermute | solution.py:21
  17.7 8.1 %collective-permute-start.3 = (f32[8,8,1,128]{3,2,1,0:T(1,128)S(1)}, f32[8,8,1,128]{3,2,1,0:T(1,128)S(1)}, u32[]{:S(2)}, u32[]{:S(2)}) collective-permute-start(f32[8,8,1,128]{3,2,1,0:T(1,128)S(1)} %get-tuple-element.76), channel_id=1, source_target_pairs={{0,8},{8,16},{16,24},{24,32},{32,40},{40,48},{48,56},{1,9},{9,17},... | collective-permute-start | bytes 98312 | tf_op jit(solution)/shard_map/ppermute | solution.py:20
  20.8 8.0 %collective-permute-start = (f32[8,1,32,128]{3,2,1,0:T(8,128)S(1)}, f32[8,1,32,128]{3,2,1,0:T(8,128)S(1)}, u32[]{:S(2)}, u32[]{:S(2)}) collective-permute-start(f32[8,1,32,128]{3,2,1,0:T(8,128)S(1)} %copy-done.6), channel_id=1, source_target_pairs={{64,0},{128,64},{192,128},{65,1},{129,65},{193,129},{66,2},{130,66... | collective-permute-start | bytes 393224 | tf_op jit(solution)/shard_map/ppermute | solution.py:21
  25.8 3.0 %copy-start.2 = (f32[8,8,32,1]{3,2,1,0:T(8,128)S(1)}, f32[8,8,32,1]{3,2,1,0:T(8,128)}, u32[]{:S(2)}) copy-start(f32[8,8,32,1]{3,2,1,0:T(8,128)} %copy.60) | copy-start | bytes 24580
  25.8 3.0 %copy-start.4 = (f32[8,8,32,1]{3,2,1,0:T(8,128)S(1)}, f32[8,8,32,1]{3,2,1,0:T(8,128)}, u32[]{:S(2)}) copy-start(f32[8,8,32,1]{3,2,1,0:T(8,128)} %copy.61) | copy-start | bytes 24580
  88.8 26.3 %collective-permute-start.7 = (f32[8,1,32,128]{3,2,1,0:T(8,128)}, f32[8,1,32,128]{3,2,1,0:T(8,128)S(1)}, u32[]{:S(2)}, u32[]{:S(2)}) collective-permute-start(f32[8,1,32,128]{3,2,1,0:T(8,128)} %get-tuple-element.73), channel_id=1, source_target_pairs={{0,64},{64,128},{128,192},{1,65},{65,129},{129,193},{2,66},{66,130... | collective-permute-start | bytes 393224 | tf_op jit(solution)/shard_map/ppermute | solution.py:20
  92.8 14.7 %collective-permute-start.10 = (f32[8,8,32,1]{2,1,3,0:T(8,128)S(1)}, f32[8,8,32,1]{2,1,3,0:T(8,128)}, u32[]{:S(2)}, u32[]{:S(2)}) collective-permute-start(f32[8,8,32,1]{2,1,3,0:T(8,128)S(1)} %copy.58), channel_id=1, source_target_pairs={{1,0},{2,1},{3,2},{4,3},{5,4},{6,5},{7,6},{9,8},{10,9},{11,10},{12... | collective-permute-start | bytes 24584 | tf_op jit(solution)/shard_map/ppermute | solution.py:21
  96.4 14.9 %collective-permute-start.11 = (f32[8,8,32,1]{2,1,3,0:T(8,128)}, f32[8,8,32,1]{2,1,3,0:T(8,128)}, u32[]{:S(2)}, u32[]{:S(2)}) collective-permute-start(f32[8,8,32,1]{2,1,3,0:T(8,128)} %copy.59), channel_id=1, source_target_pairs={{0,1},{1,2},{2,3},{3,4},{4,5},{5,6},{6,7},{8,9},{9,10},{10,11},{11... | collective-permute-start | bytes 24584 | tf_op jit(solution)/shard_map/ppermute | solution.py:20
  101.5 11.9 %collective-permute-start.8 = (f32[8,8,1,128]{3,2,1,0:T(1,128)}, f32[8,8,1,128]{3,2,1,0:T(1,128)}, u32[]{:S(2)}, u32[]{:S(2)}) collective-permute-start(f32[8,8,1,128]{3,2,1,0:T(1,128)} %get-tuple-element.71), channel_id=1, source_target_pairs={{8,0},{16,8},{24,16},{32,24},{40,32},{48,40},{56,48},{9,1},{17,9},... | collective-permute-start | bytes 98312 | tf_op jit(solution)/shard_map/ppermute | solution.py:21
  103.5 10.8 %collective-permute-start.9 = (f32[8,8,1,128]{3,2,1,0:T(1,128)}, f32[8,8,1,128]{3,2,1,0:T(1,128)}, u32[]{:S(2)}, u32[]{:S(2)}) collective-permute-start(f32[8,8,1,128]{3,2,1,0:T(1,128)} %get-tuple-element.70), channel_id=1, source_target_pairs={{0,8},{8,16},{16,24},{24,32},{32,40},{40,48},{48,56},{1,9},{9,17},... | collective-permute-start | bytes 98312 | tf_op jit(solution)/shard_map/ppermute | solution.py:20
  107.6 8.2 %collective-permute-start.6 = (f32[8,1,32,128]{3,2,1,0:T(8,128)}, f32[8,1,32,128]{3,2,1,0:T(8,128)S(1)}, u32[]{:S(2)}, u32[]{:S(2)}) collective-permute-start(f32[8,1,32,128]{3,2,1,0:T(8,128)} %get-tuple-element.72), channel_id=1, source_target_pairs={{64,0},{128,64},{192,128},{65,1},{129,65},{193,129},{66,2},{130,66... | collective-permute-start | bytes 393224 | tf_op jit(solution)/shard_map/ppermute | solution.py:21
  115.1 1.2 copy-start.1
  115.1 1.5 copy-start.3
where the time goes:
time: 175 us; the launch traced here: 174 us
  blocking collectives  79.4 us (45%)
  local copies, waits for them, and re-layouts  30.8 us (18%)
  starting transfers between devices  28.9 us (17%)
  other arithmetic  16.5 us (9%)
  matrix products  14.1 us (8%)
  waiting for transfers between devices  3.37 us (2%)
    psum x8, blocking collectives, by_axis(): value = lax.psum(value, axis)  79.4 us
    ppermute x6, starting transfers between devices, padded_2(): lax.ppermute(last, axis, up)  19.7 us
    unnamed x30, local copies, waits for them, and re-layouts  18.2 us
    dot_general x16, matrix products, small_dot(): return jnp.dot(left, right, precision=lax.Precision.HIGHEST)  13.3 us
    ppermute x6, starting transfers between devices, padded_2(): lax.ppermute(leading, axis, [(b, a) for a, b in up])  9.2 us
    slice x4, local copies, waits for them, and re-layouts, padded_2(): leading = lax.slice_in_dim(value, 0, width, axis=dim)  6.01 us
    another operation x5, other arithmetic  3.95 us
  transfers between devices with their start and end apart: 12, of which 2 were waited for; matrix products, arithmetic and copies ran while one was open for 12% of the time, Pallas kernels for 0%

commit v1 on v0

v1 whole, which is shorter than its diff:
```python
import functools

import jax
import jax.numpy as jnp
from jax import lax
from jax.experimental import pallas as pl
from jax.experimental.pallas import tpu as pltpu
from jax.sharding import PartitionSpec as P

MESH = pl.DeviceIdType.MESH
F, NX, NY, NZ = 8, 8, 32, 128
TOP = 8
ROWS = slice(TOP, TOP + NY)
GROUPS = 4
WIDE = F // GROUPS
TILE = (8, 128)


def exchange_kernel(gx, gy, gz, b_hbm, s_hbm, gram_ref, ab_hbm,
                    buf_p, buf_q, buf_r, diag, side, pack_s, pack_r, part_z, part_p,
                    load_sem, xs_sem, xr_sem, ys_sem, yr_sem, zs_sem, zr_sem,
                    g_send, g_recv, out_sem):
    ix, iy, iz = lax.axis_index("gx"), lax.axis_index("gy"), lax.axis_index("gz")
    plane = gx * gy
    here = ix * gy + iy

    def in_plane(k):
        other = lax.rem(here + k, plane)
        return (lax.div(other, gy), lax.rem(other, gy), iz)

    def in_line(k):
        return (ix, iy, lax.rem(iz + k, gz))

    barrier = pltpu.get_barrier_semaphore()
    for k in range(1, gz):
        pl.semaphore_signal(barrier, inc=1, device_id=in_line(k), device_id_type=MESH)
    for k in range(1, plane):
        pl.semaphore_signal(barrier, inc=1, device_id=in_plane(k), device_id_type=MESH)

    loads = [
        pltpu.make_async_copy(b_hbm.at[:, 0], buf_p.at[:, 1, ROWS], load_sem.at[0]),
        pltpu.make_async_copy(b_hbm.at[:, NX - 1], buf_p.at[:, NX, ROWS], load_sem.at[1]),
        pltpu.make_async_copy(b_hbm.at[:, 1:NX - 1], buf_p.at[:, 2:NX, ROWS], load_sem.at[2]),
        pltpu.make_async_copy(s_hbm, diag, load_sem.at[3]),
    ]
    for load in loads:
        load.start()

    zero_x = jnp.zeros((F, NY, NZ), jnp.float32)
    zero_y = jnp.zeros((F, NX, 1, NZ), jnp.float32)
    zero_z = jnp.zeros((2 * F, NZ), jnp.float32)
    for turn, buf in enumerate((buf_p, buf_q)):
        @pl.when(ix == 0)
        def _():
            buf[:, 0, ROWS] = zero_x

        @pl.when(ix == gx - 1)
        def _():
            buf[:, NX + 1, ROWS] = zero_x

        @pl.when(iy == 0)
        def _():
            buf[:, 1:NX + 1, TOP - 1:TOP] = zero_y

        @pl.when(iy == gy - 1)
        def _():
            buf[:, 1:NX + 1, TOP + NY:TOP + NY + 1] = zero_y

        @pl.when(iz == 0)
        def _():
            pack_r[turn, 0] = zero_z

        @pl.when(iz == gz - 1)
        def _():
            pack_r[turn, 1] = zero_z

    bufs = (buf_p, buf_q)
    has = {
        "x": (ix > 0, ix < gx - 1),
        "y": (iy > 0, iy < gy - 1),
        "z": (iz > 0, iz < gz - 1),
    }

    def x_copy(turn, way, group):
        fields = slice(group * WIDE, (group + 1) * WIDE)
        buf = bufs[turn]
        return pltpu.make_async_remote_copy(
            src_ref=buf.at[fields, NX if way else 1, ROWS],
            dst_ref=buf.at[fields, 0 if way else NX + 1, ROWS],
            send_sem=xs_sem.at[turn, way, group],
            recv_sem=xr_sem.at[turn, way, group],
            device_id=(ix + 1 if way else ix - 1, iy, iz),
            device_id_type=MESH,
        )

    def y_copy(turn, way):
        buf = bufs[turn]
        src, dst = (TOP + NY - 1, TOP - 1) if way else (TOP, TOP + NY)
        return pltpu.make_async_remote_copy(
            src_ref=buf.at[:, 1:NX + 1, src:src + 1],
            dst_ref=buf.at[:, 1:NX + 1, dst:dst + 1],
            send_sem=ys_sem.at[turn, way],
            recv_sem=yr_sem.at[turn, way],
            device_id=(ix, iy + 1 if way else iy - 1, iz),
            device_id_type=MESH,
        )

    def z_copy(turn, way):
        return pltpu.make_async_remote_copy(
            src_ref=pack_s.at[turn, way],
            dst_ref=pack_r.at[turn, 0 if way else 1],
            send_sem=zs_sem.at[turn, way],
            recv_sem=zr_sem.at[turn, way],
            device_id=(ix, iy, iz + 1 if way else iz - 1),
            device_id_type=MESH,
        )

    def start(axis, way, copy):
        @pl.when(has[axis][way])
        def _():
            copy.start()

    def arrive(axis, way, copy):
        @pl.when(has[axis][1 - way])
        def _():
            copy.wait_recv()

    def sent(axis, way, copy):
        @pl.when(has[axis][way])
        def _():
            copy.wait_send()

    def pack_z(turn):
        buf = bufs[turn]
        for t in range(2 * F):
            f, half = t // 2, t % 2
            tile = buf[f, 1 + 4 * half:5 + 4 * half, ROWS].reshape(NZ, NZ).T
            pack_s[turn, 0, t:t + 1] = tile[0:1]
            pack_s[turn, 1, t:t + 1] = tile[NZ - 1:NZ]

    def unpack_z(turn):
        for t in range(2 * F):
            f, half = t // 2, t % 2
            low = jnp.broadcast_to(pack_r[turn, 0, t:t + 1], (NZ // 2, NZ))
            high = jnp.broadcast_to(pack_r[turn, 1, t:t + 1], (NZ // 2, NZ))
            tile = jnp.concatenate([low, high], axis=0).T
            side[f, 4 * half:4 * half + 4] = tile.reshape(4, NY, NZ)

    lane = lax.broadcasted_iota(jnp.int32, (NY, NZ), 1)
    first, last = lane == 0, lane == NZ - 1

    def apply(src, f, x):
        c = src[f, x, ROWS]
        edge = side[f, x - 1]
        beside = src[f, x + 1, ROWS] + src[f, x - 1, ROWS]
        beside = beside + src[f, x, TOP + 1:TOP + NY + 1] + src[f, x, TOP - 1:TOP + NY - 1]
        up = jnp.where(last, edge, pltpu.roll(c, NZ - 1, 1))
        down = jnp.where(first, edge, pltpu.roll(c, 1, 1))
        beside = beside + up + down
        return (6.0 + diag[x - 1]) * c - beside

    def at_p(x, rows):
        return buf_p[:, x, rows]

    def at_q(x, rows):
        return buf_q[:, x, rows]

    def at_r(x, rows):
        return buf_r[:, x, rows]

    def moment(left, right, low, high, sums):
        def step(x, sums):
            for t in range(NY // 8):
                rows = slice(TOP + 8 * t, TOP + 8 * t + 8)
                u = left(x, rows)
                v = u if right is left else right(x, rows)
                sums = tuple(sums[i] + u[i:i + 1] * v[i:] for i in range(F))
            return sums

        return lax.fori_loop(low, high, step, sums)

    none = tuple(jnp.zeros((F - i,) + TILE, jnp.float32) for i in range(F))

    sub = lax.broadcasted_iota(jnp.int32, TILE, 0)
    cell = lax.broadcasted_iota(jnp.int32, TILE, 1)

    def fold(parts):
        width = 1
        while len(parts) > 1:
            odd = (sub & width) != 0
            merged = []
            for i in range(0, len(parts), 2):
                a, b = parts[i], parts[i + 1]
                kept = jnp.where(odd, b, a)
                moved = jnp.where(odd, a, b)
                moved = jnp.where(odd, pltpu.roll(moved, width, 0), pltpu.roll(moved, 8 - width, 0))
                merged.append(kept + moved)
            parts = merged
            width *= 2
        return parts[0]

    def gather(order, sums, total):
        for c in range(F):
            row = fold([sums[min(i, c)][max(i, c) - min(i, c)] for i in range(F)])
            total = jnp.where(cell == order * F + c, jnp.sum(row, axis=1, keepdims=True), total)
        return total

    loads[0].wait()
    loads[1].wait()
    pl.semaphore_wait(barrier, gz - 1 + plane - 1)
    for group in range(GROUPS):
        for way in range(2):
            start("x", way, x_copy(0, way, group))
    loads[2].wait()
    for way in range(2):
        start("y", way, y_copy(0, way))
    pack_z(0)
    for way in range(2):
        start("z", way, z_copy(0, way))
    loads[3].wait()
    total = gather(0, moment(at_p, at_p, 1, NX + 1, none), jnp.zeros(TILE, jnp.float32))
    for way in range(2):
        arrive("y", way, y_copy(0, way))
        arrive("z", way, z_copy(0, way))
    unpack_z(0)

    def inner(src, dst, shift):
        def step(f, _):
            for x in range(2, NX):
                dst[f, x, ROWS] = apply(src, f, x)
            return 0

        lax.fori_loop(0, F, step, 0)

    inner(buf_p, buf_q, 0)

    def outer(src, dst, turn):
        for group in range(GROUPS):
            for way in range(2):
                arrive("x", way, x_copy(turn, way, group))
            for f in range(group * WIDE, (group + 1) * WIDE):
                for x in (1, NX):
                    dst[f, x, ROWS] = apply(src, f, x)
            if turn == 0:
                for way in range(2):
                    start("x", way, x_copy(1, way, group))

    outer(buf_p, buf_q, 0)

    for way in range(2):
        start("y", way, y_copy(1, way))
    pack_z(1)
    for way in range(2):
        start("z", way, z_copy(1, way))
    out_copy = pltpu.make_async_copy(buf_q.at[:, 1:NX + 1, ROWS], ab_hbm, out_sem.at[0])
    out_copy.start()
    total = gather(1, moment(at_p, at_q, 1, NX + 1, none), total)
    total = gather(2, moment(at_q, at_q, 1, NX + 1, none), total)
    for way in range(2):
        arrive("y", way, y_copy(1, way))
        arrive("z", way, z_copy(1, way))
    unpack_z(1)
    inner(buf_q, buf_r, 0)
    third = moment(at_q, at_r, 2, NX, none)
    fourth = moment(at_r, at_r, 2, NX, none)
    outer(buf_q, buf_r, 1)
    for x in (1, NX):
        third = moment(at_q, at_r, x, x + 1, third)
        fourth = moment(at_r, at_r, x, x + 1, fourth)
    total = gather(3, third, total)
    total = gather(4, fourth, total)

    def line_copy(k):
        return pltpu.make_async_remote_copy(
            src_ref=part_z.at[iz], dst_ref=part_z.at[iz],
            send_sem=g_send.at[0], recv_sem=g_recv.at[0],
            device_id=in_line(k), device_id_type=MESH)

    def plane_copy(k):
        return pltpu.make_async_remote_copy(
            src_ref=part_p.at[here], dst_ref=part_p.at[here],
            send_sem=g_send.at[1], recv_sem=g_recv.at[1],
            device_id=in_plane(k), device_id_type=MESH)

    part_z[iz] = total
    for k in range(1, gz):
        line_copy(k).start()
    every = pltpu.make_async_remote_copy(
        src_ref=part_z.at[0:gz - 1], dst_ref=part_z.at[0:gz - 1],
        send_sem=g_send.at[0], recv_sem=g_recv.at[0],
        device_id=in_line(1), device_id_type=MESH)
    every.wait_recv()
    total = part_z[0]
    for k in range(1, gz):
        total = total + part_z[k]
    part_p[here] = total
    for k in range(1, plane):
        plane_copy(k).start()
    most = pltpu.make_async_remote_copy(
        src_ref=part_p.at[0:plane - 1], dst_ref=part_p.at[0:plane - 1],
        send_sem=g_send.at[1], recv_sem=g_recv.at[1],
        device_id=in_plane(1), device_id_type=MESH)
    most.wait_recv()
    total = part_p[0]
    for k in range(1, plane):
        total = total + part_p[k]
    gram_ref[...] = total

    every.wait_send()
    most.wait_send()
    for turn in range(2):
        for way in range(2):
            for group in range(GROUPS):
                sent("x", way, x_copy(turn, way, group))
            sent("y", way, y_copy(turn, way))
            sent("z", way, z_copy(turn, way))
    out_copy.wait()


def combine_kernel(gram_ref, b_hbm, ab_hbm, x_hbm, norm_ref, buf_b, buf_a, buf_x, coeff, load_sem, out_sem):
    load_b = pltpu.make_async_copy(b_hbm, buf_b, load_sem.at[0])
    load_a = pltpu.make_async_copy(ab_hbm, buf_a, load_sem.at[1])
    load_b.start()
    load_a.start()

    gram = gram_ref[...]
    sub = lax.broadcasted_iota(jnp.int32, TILE, 0)
    cell = lax.broadcasted_iota(jnp.int32, TILE, 1)

    def column(order, c):
        k = order * F + c
        return jnp.broadcast_to(gram[:, k:k + 1], TILE)

    def spread(value, row):
        return jnp.broadcast_to(value[row:row + 1], TILE)

    moments = [[column(order, c) for c in range(F)] for order in range(5)]
    columns = [[moments[2][c], moments[3][c]] for c in range(F)]
    columns += [[moments[3][c], moments[4][c]] for c in range(F)]
    rights = [[moments[1][c], moments[2][c]] for c in range(F)]
    for k in range(2 * F):
        half, row = k // F, k % F
        pivot = columns[k]
        inverse = 1.0 / spread(pivot[half], row)
        mine = sub == row
        for other in columns[k + 1:] + rights:
            r = spread(other[half], row) * inverse
            for h in range(2):
                value = other[h] - pivot[h] * r
                other[h] = jnp.where(mine, r, value) if h == half else value
    norms = jnp.zeros((1, 128), jnp.float32)
    for c in range(F):
        for h in range(2):
            coeff[c, h] = rights[c][h]
        fit = moments[1][c] * rights[c][0] + moments[2][c] * rights[c][1]
        left = jnp.where(sub == c, moments[0][c], 0.0) - fit
        norms = jnp.where(cell[0:1] == c, jnp.sum(left, axis=0, keepdims=True), norms)
    norm_ref[...] = jnp.sqrt(jnp.maximum(norms, 0.0))[:, :F]

    load_b.wait()
    load_a.wait()
    pair = 2
    outs = []
    for c0 in range(0, F, pair):
        weights = [[[spread(coeff[c, h], i) for i in range(F)] for h in range(2)] for c in range(c0, c0 + pair)]

        def step(x, _):
            for t in range(NY // 8):
                rows = slice(8 * t, 8 * t + 8)
                fields = [buf_b[:, x, rows], buf_a[:, x, rows]]
                for c in range(pair):
                    sums = [None, None]
                    for h in range(2):
                        for i in range(F):
                            term = weights[c][h][i] * fields[h][i]
                            sums[h] = term if sums[h] is None else sums[h] + term
                    buf_x[c0 + c, x, rows] = sums[0] + sums[1]
            return 0

        lax.fori_loop(0, NX, step, 0)
        out = pltpu.make_async_copy(buf_x.at[c0:c0 + pair], x_hbm.at[c0:c0 + pair], out_sem.at[c0 // pair])
        out.start()
        outs.append(out)
    for out in outs:
        out.wait()


def solution(mesh):
    gx, gy, gz = mesh.shape["gx"], mesh.shape["gy"], mesh.shape["gz"]
    f32 = jnp.float32
    dma = pltpu.SemaphoreType.DMA
    anywhere = pl.BlockSpec(memory_space=pl.ANY)
    vmem = pl.BlockSpec(memory_space=pltpu.VMEM)
    block = (F, NX, NY, NZ)
    padded = (F, NX + 2, NY + 16, NZ)

    def body(right_side, shift):
        gram, images = pl.pallas_call(
            functools.partial(exchange_kernel, gx, gy, gz),
            out_shape=(jax.ShapeDtypeStruct(TILE, f32), jax.ShapeDtypeStruct(block, f32)),
            in_specs=[anywhere, anywhere],
            out_specs=(vmem, anywhere),
            scratch_shapes=[
                pltpu.VMEM(padded, f32),
                pltpu.VMEM(padded, f32),
                pltpu.VMEM(padded, f32),
                pltpu.VMEM((NX, NY, NZ), f32),
                pltpu.VMEM(block, f32),
                pltpu.VMEM((2, 2, 2 * F, NZ), f32),
                pltpu.VMEM((2, 2, 2 * F, NZ), f32),
                pltpu.VMEM((gz,) + TILE, f32),
                pltpu.VMEM((gx * gy,) + TILE, f32),
                dma((4,)),
                dma((2, 2, GROUPS)),
                dma((2, 2, GROUPS)),
                dma((2, 2)),
                dma((2, 2)),
                dma((2, 2)),
                dma((2, 2)),
                dma((2,)),
                dma((2,)),
                dma((1,)),
            ],
            compiler_params=pltpu.CompilerParams(
                collective_id=0, has_side_effects=True, vmem_limit_bytes=24 << 20
            ),
        )(right_side, shift)
        solved, norms = pl.pallas_call(
            combine_kernel,
            out_shape=(jax.ShapeDtypeStruct(block, f32), jax.ShapeDtypeStruct((1, F), f32)),
            in_specs=[vmem, anywhere, anywhere],
            out_specs=(anywhere, vmem),
            scratch_shapes=[
                pltpu.VMEM(block, f32),
                pltpu.VMEM(block, f32),
                pltpu.VMEM(block, f32),
                pltpu.VMEM((F, 2) + TILE, f32),
                dma((2,)),
                dma((F // 2,)),
            ],
            compiler_params=pltpu.CompilerParams(vmem_limit_bytes=16 << 20),
        )(gram, right_side, images)
        return solved, norms.reshape(F)

    return jax.shard_map(
        body,
        mesh=mesh,
        in_specs=(P(None, "gx", "gy", "gz"), P("gx", "gy", "gz")),
        out_specs=(P(None, "gx", "gy", "gz"), P()),
        check_vma=False,
    )
```

time: 175 us -> 38.2 us (0.22)
  the two profiles are of different devices: /device:TPU:8 before, /device:TPU:1 now
where the time goes in v1:
time: 38.2 us; the launch traced here: 38.1 us
  Pallas kernels  35.3 us (92%)
  local copies, waits for them, and re-layouts  2.12 us (6%)
  between operations  0.65 us (2%)
    pallas_call x1, Pallas kernels, body(): pl.pallas_call(functools.partial(exchange_kernel, gx, gy, gz), out_shape=...  32.1 us
    pallas_call x1, Pallas kernels, body(): pl.pallas_call(combine_kernel, out_shape=(jax.ShapeDtypeStruct(block, f32...  3.22 us
    unnamed x4, local copies, waits for them, and re-layouts  2.12 us

profile of v1, /device:TPU:1, one launch (start us, length us, event | category | flops | bytes accessed | tf_op | source)
XLA Modules:
  0.0 38.1 jit_solution(15552608226198261824)
XLA Ops:
  0.6 0.0 copy-start
  0.6 1.2 %copy-done = f32[8,8,32,128]{3,2,1,0:T(8,128)S(1)} copy-done((f32[8,8,32,128]{3,2,1,0:T(8,128)S(1)}, f32[8,8,32,128]{3,2,1,0:T(8,128)}, u32[]{:S(2)}) %copy-start) | copy-done | bytes 1048600
  1.9 0.0 copy-start.1
  1.9 0.9 %copy-done.1 = f32[8,32,128]{2,1,0:T(8,128)S(1)} copy-done((f32[8,32,128]{2,1,0:T(8,128)S(1)}, f32[8,32,128]{2,1,0:T(8,128)}, u32[]{:S(2)}) %copy-start.1) | copy-done | bytes 131096
  2.8 32.1 %shard_map.41 = (f32[8,128]{1,0:T(8,128)S(1)}, f32[8,8,32,128]{3,2,1,0:T(8,128)S(1)}) custom-call(f32[8,8,32,128]{3,2,1,0:T(8,128)S(1)} %copy-done, f32[8,32,128]{2,1,0:T(8,128)S(1)} %copy-done.1), custom_call_target="tpu_custom_call" | custom-call | tf_op jit(solution)/shard_map/pallas_call | solution.py:398
  34.8 3.2 %shard_map.42 = (f32[8,8,32,128]{3,2,1,0:T(8,128)}, f32[1,8]{1,0:T(1,128)}) custom-call(f32[8,128]{1,0:T(8,128)S(1)} %get-tuple-element.6.gram_ref, f32[8,8,32,128]{3,2,1,0:T(8,128)S(1)} %copy-done, f32[8,8,32,128]{3,2,1,0:T(8,128)S(1)} %get-tuple-element.7.ab_hbm), custom_call_target="tpu_custom_call" | custom-call | tf_op jit(solution)/shard_map/pallas_call | solution.py:428
Async XLA Ops:
  0.6 1.2 %copy-start = (f32[8,8,32,128]{3,2,1,0:T(8,128)S(1)}, f32[8,8,32,128]{3,2,1,0:T(8,128)}, u32[]{:S(2)}) copy-start(f32[8,8,32,128]{3,2,1,0:T(8,128)} %b_hbm.3) | copy-start | bytes 3145732
  1.9 0.9 %copy-start.1 = (f32[8,32,128]{2,1,0:T(8,128)S(1)}, f32[8,32,128]{2,1,0:T(8,128)}, u32[]{:S(2)}) copy-start(f32[8,32,128]{2,1,0:T(8,128)} %s_hbm.1) | copy-start | bytes 393220

commit v2 on v1

v2 whole, which is shorter than its diff:
```python
import functools

import jax
import jax.numpy as jnp
from jax import lax
from jax.experimental import pallas as pl
from jax.experimental.pallas import tpu as pltpu
from jax.sharding import PartitionSpec as P

MESH = pl.DeviceIdType.MESH
F, NX, NY, NZ = 8, 8, 32, 128
TOP = 8
ROWS = slice(TOP, TOP + NY)
GROUPS = 4
WIDE = F // GROUPS
INNER, FACE = 12, 4
TILE = (8, 128)


def exchange_kernel(gx, gy, gz, b_hbm, s_hbm, gram_ref, buf_p, buf_q,
                    buf_r, diag, side, inner_s, inner_r, face_s, face_r, part_z, part_p,
                    load_sem, xs_sem, xr_sem, ys_sem, yr_sem, zs_sem, zr_sem, g_send, g_recv):
    ix, iy, iz = lax.axis_index("gx"), lax.axis_index("gy"), lax.axis_index("gz")

    loads = [
        pltpu.make_async_copy(b_hbm.at[:, 0], buf_p.at[:, 1, ROWS], load_sem.at[0]),
        pltpu.make_async_copy(b_hbm.at[:, NX - 1], buf_p.at[:, NX, ROWS], load_sem.at[1]),
        pltpu.make_async_copy(b_hbm.at[:, 1:NX - 1], buf_p.at[:, 2:NX, ROWS], load_sem.at[2]),
        pltpu.make_async_copy(s_hbm, diag, load_sem.at[3]),
    ]
    for load in loads:
        load.start()

    chips_y = gy // 2
    core = lax.rem(iy, 2)
    row = iy - core
    xs = [ix] + [lax.rem(ix + k, gx) for k in range(1, gx)]
    ys = [iy] + [lax.rem(iy + 2 * k, gy) for k in range(1, chips_y)]
    zs = [iz] + [lax.rem(iz + k, gz) for k in range(1, gz)]
    across = row + 1 - core
    beyond = lax.rem(iy + gy - 1 + 2 * core, gy)
    line = [(ix, y, zs[k]) for k in dict.fromkeys((1, gz - 1) + tuple(range(2, gz - 1))) for y in (iy, across)]
    line = [(ix, across, iz)] + line
    plane = [(xs[a], ys[b], iz) for a in range(gx) for b in range(chips_y) if a or b]
    near = [(xs[k], iy, iz) for k in dict.fromkeys((1, gx - 1))] + [(ix, beyond, iz)]
    rest = [(xs[a], ys[b], iz) for a in range(gx) for b in range(chips_y) if (a or b) and not (b == 0 and a in (1, gx - 1))]
    greeted = near + line + rest

    barrier = pltpu.get_barrier_semaphore()
    for device in greeted:
        pl.semaphore_signal(barrier, inc=1, device_id=device, device_id_type=MESH)

    zero_x = jnp.zeros((F, NY, NZ), jnp.float32)
    zero_y = jnp.zeros((F, NX, 1, NZ), jnp.float32)
    for turn, buf in enumerate((buf_p, buf_q)):
        @pl.when(ix == 0)
        def _():
            buf[:, 0, ROWS] = zero_x

        @pl.when(ix == gx - 1)
        def _():
            buf[:, NX + 1, ROWS] = zero_x

        @pl.when(iy == 0)
        def _():
            buf[:, 1:NX + 1, TOP - 1:TOP] = zero_y

        @pl.when(iy == gy - 1)
        def _():
            buf[:, 1:NX + 1, TOP + NY:TOP + NY + 1] = zero_y

        for way, edge in enumerate((0, gz - 1)):
            @pl.when(iz == edge)
            def _():
                inner_r[turn, way] = jnp.zeros((INNER, NZ), jnp.float32)
                face_r[turn, way] = jnp.zeros((FACE, NZ), jnp.float32)

    bufs = (buf_p, buf_q)
    has = {
        "x": (ix > 0, ix < gx - 1),
        "y": (iy > 0, iy < gy - 1),
        "z": (iz > 0, iz < gz - 1),
    }

    def x_copy(turn, way, group):
        fields = slice(group * WIDE, (group + 1) * WIDE)
        buf = bufs[turn]
        return pltpu.make_async_remote_copy(
            src_ref=buf.at[fields, NX if way else 1, ROWS],
            dst_ref=buf.at[fields, 0 if way else NX + 1, ROWS],
            send_sem=xs_sem.at[turn, way, group],
            recv_sem=xr_sem.at[turn, way, group],
            device_id=(ix + 1 if way else ix - 1, iy, iz),
            device_id_type=MESH,
        )

    planes = (slice(2, NX), slice(1, 2), slice(NX, NX + 1))

    def y_copy(turn, way, part):
        buf = bufs[turn]
        src, dst = (TOP + NY - 1, TOP - 1) if way else (TOP, TOP + NY)
        return pltpu.make_async_remote_copy(
            src_ref=buf.at[:, planes[part], src:src + 1],
            dst_ref=buf.at[:, planes[part], dst:dst + 1],
            send_sem=ys_sem.at[turn, way, part],
            recv_sem=yr_sem.at[turn, way, part],
            device_id=(ix, iy + 1 if way else iy - 1, iz),
            device_id_type=MESH,
        )

    def z_copy(turn, way, part):
        source, target = ((inner_s, inner_r), (face_s, face_r))[part]
        return pltpu.make_async_remote_copy(
            src_ref=source.at[turn, way],
            dst_ref=target.at[turn, 0 if way else 1],
            send_sem=zs_sem.at[turn, way, part],
            recv_sem=zr_sem.at[turn, way, part],
            device_id=(ix, iy, iz + 1 if way else iz - 1),
            device_id_type=MESH,
        )

    def start(axis, way, copies):
        @pl.when(has[axis][way])
        def _():
            for copy in copies:
                copy.start()

    def arrive(axis, way, copies):
        @pl.when(has[axis][1 - way])
        def _():
            for copy in copies:
                copy.wait_recv()

    def sent(axis, way, copies):
        @pl.when(has[axis][way])
        def _():
            for copy in copies:
                copy.wait_send()

    tiles = ([], [])
    for f in range(0, F, 2):
        tiles[0].append([(f, 2, 6)])
        tiles[0].append([(f, 6, 8), (f + 1, 2, 4)])
        tiles[0].append([(f + 1, 4, 8)])
        tiles[1].append([(f, 1, 2), (f, 8, 9), (f + 1, 1, 2), (f + 1, 8, 9)])

    def pack_z(turn, part):
        buf, target = bufs[turn], (inner_s, face_s)[part]
        for t, pieces in enumerate(tiles[part]):
            tile = jnp.concatenate([buf[f, a:b, ROWS] for f, a, b in pieces], axis=0)
            tile = tile.reshape(NZ, NZ).T
            target[turn, 0, t:t + 1] = tile[0:1]
            target[turn, 1, t:t + 1] = tile[NZ - 1:NZ]

    def unpack_z(turn, part):
        source = (inner_r, face_r)[part]
        for t, pieces in enumerate(tiles[part]):
            low = jnp.broadcast_to(source[turn, 0, t:t + 1], (NZ // 2, NZ))
            high = jnp.broadcast_to(source[turn, 1, t:t + 1], (NZ // 2, NZ))
            tile = jnp.concatenate([low, high], axis=0).T.reshape(4, NY, NZ)
            at = 0
            for f, a, b in pieces:
                side[f, a - 1:b - 1] = tile[at:at + b - a]
                at += b - a

    lane = lax.broadcasted_iota(jnp.int32, (NY, NZ), 1)
    first, last = lane == 0, lane == NZ - 1

    def apply(src, dst, f, x):
        c = src[f, x, ROWS]
        edge = side[f, x - 1]
        beside = src[f, x + 1, ROWS] + src[f, x - 1, ROWS]
        beside = beside + src[f, x, TOP + 1:TOP + NY + 1] + src[f, x, TOP - 1:TOP + NY - 1]
        up = jnp.where(last, edge, pltpu.roll(c, NZ - 1, 1))
        down = jnp.where(first, edge, pltpu.roll(c, 1, 1))
        beside = beside + up + down
        dst[f, x, ROWS] = (6.0 + diag[x - 1]) * c - beside

    def moment(left, right, low, high, sums):
        def step(x, sums):
            for t in range(NY // 8):
                rows = slice(TOP + 8 * t, TOP + 8 * t + 8)
                u = left[:, x, rows]
                v = u if right is left else right[:, x, rows]
                sums = tuple(sums[i] + u[i:i + 1] * v[i:] for i in range(F))
            return sums

        return lax.fori_loop(low, high, step, sums)

    def faces(left, right, sums):
        def step(k, sums):
            x = 1 + (NX - 1) * k
            for t in range(NY // 8):
                rows = slice(TOP + 8 * t, TOP + 8 * t + 8)
                u = left[:, x, rows]
                v = u if right is left else right[:, x, rows]
                sums = tuple(sums[i] + u[i:i + 1] * v[i:] for i in range(F))
            return sums

        return lax.fori_loop(0, 2, step, sums)

    none = tuple(jnp.zeros((F - i,) + TILE, jnp.float32) for i in range(F))

    sub = lax.broadcasted_iota(jnp.int32, TILE, 0)
    cell = lax.broadcasted_iota(jnp.int32, TILE, 1)

    def fold(parts):
        width = 1
        while len(parts) > 1:
            odd = (sub & width) != 0
            merged = []
            for i in range(0, len(parts), 2):
                a, b = parts[i], parts[i + 1]
                kept = jnp.where(odd, b, a)
                moved = jnp.where(odd, a, b)
                moved = jnp.where(odd, pltpu.roll(moved, width, 0), pltpu.roll(moved, 8 - width, 0))
                merged.append(kept + moved)
            parts = merged
            width *= 2
        return parts[0]

    def gather(order, sums, total):
        for c in range(F):
            line = fold([sums[min(i, c)][max(i, c) - min(i, c)] for i in range(F)])
            total = jnp.where(cell == order * F + c, jnp.sum(line, axis=1, keepdims=True), total)
        return total

    def inner(src, dst):
        def step(f, _):
            for x in range(2, NX):
                apply(src, dst, f, x)
            return 0

        lax.fori_loop(0, F, step, 0)

    def outer(src, dst, turn, group):
        for way in range(2):
            arrive("x", way, [x_copy(turn, way, group)])
        for f in range(group * WIDE, (group + 1) * WIDE):
            for x in (1, NX):
                apply(src, dst, f, x)
        if turn == 0:
            for way in range(2):
                start("x", way, [x_copy(1, way, group)])

    both = range(2)
    loads[0].wait()
    loads[1].wait()
    pl.semaphore_wait(barrier, len(greeted))
    for way in both:
        start("x", way, [x_copy(0, way, group) for group in range(GROUPS)])
    loads[2].wait()
    for way in both:
        start("y", way, [y_copy(0, way, part) for part in range(3)])
    for part in both:
        pack_z(0, part)
    for way in both:
        start("z", way, [z_copy(0, way, part) for part in both])
    loads[3].wait()
    zeroth = moment(buf_p, buf_p, 1, NX + 1, none)
    total = gather(0, zeroth, jnp.zeros(TILE, jnp.float32))
    for way in both:
        arrive("y", way, [y_copy(0, way, part) for part in range(3)])
        arrive("z", way, [z_copy(0, way, part) for part in both])
    for part in both:
        unpack_z(0, part)

    outer(buf_p, buf_q, 0, 0)
    inner(buf_p, buf_q)
    for way in both:
        start("y", way, [y_copy(1, way, 0)])
    pack_z(1, 0)
    for way in both:
        start("z", way, [z_copy(1, way, 0)])
    for group in range(1, GROUPS):
        outer(buf_p, buf_q, 0, group)
    for way in both:
        start("y", way, [y_copy(1, way, part) for part in (1, 2)])
    pack_z(1, 1)
    for way in both:
        start("z", way, [z_copy(1, way, 1)])
    total = gather(1, moment(buf_p, buf_q, 1, NX + 1, none), total)
    total = gather(2, moment(buf_q, buf_q, 1, NX + 1, none), total)

    for way in both:
        arrive("y", way, [y_copy(1, way, 0)])
        arrive("z", way, [z_copy(1, way, 0)])
    unpack_z(1, 0)
    inner(buf_q, buf_r)
    third = moment(buf_q, buf_r, 2, NX, none)
    fourth = moment(buf_r, buf_r, 2, NX, none)
    for way in both:
        arrive("y", way, [y_copy(1, way, part) for part in (1, 2)])
        arrive("z", way, [z_copy(1, way, 1)])
    unpack_z(1, 1)
    for group in range(GROUPS):
        outer(buf_q, buf_r, 1, group)
    third = faces(buf_q, buf_r, third)
    fourth = faces(buf_r, buf_r, fourth)
    total = gather(3, third, total)
    total = gather(4, fourth, total)

    def spread(stage, parts, mine, devices, total):
        slots = len(devices) + 1
        parts[mine] = total

        def copy(src, dst, device):
            return pltpu.make_async_remote_copy(
                src_ref=src, dst_ref=dst,
                send_sem=g_send.at[stage], recv_sem=g_recv.at[stage],
                device_id=device, device_id_type=MESH)

        for device in devices:
            copy(parts.at[mine], parts.at[mine], device).start()
        every = copy(parts.at[0:slots - 1], parts.at[0:slots - 1], devices[0])
        every.wait_recv()
        sums = [parts[k] for k in range(slots)]
        while len(sums) > 1:
            sums = [sums[k] + sums[k + 1] for k in range(0, len(sums), 2)]
        return sums[0], every

    total, lines_done = spread(0, part_z, 2 * iz + core, line, total)
    total, planes_done = spread(1, part_p, ix * chips_y + lax.div(row, 2), plane, total)
    gram_ref[...] = total

    lines_done.wait_send()
    planes_done.wait_send()
    for turn in both:
        for way in both:
            sent("x", way, [x_copy(turn, way, group) for group in range(GROUPS)])
            sent("y", way, [y_copy(turn, way, part) for part in range(3)])
            sent("z", way, [z_copy(turn, way, part) for part in both])


def combine_kernel(gram_ref, buf_b, buf_a, x_hbm, norm_ref, buf_x, coeff, out_sem):
    gram = gram_ref[...]
    sub = lax.broadcasted_iota(jnp.int32, TILE, 0)
    cell = lax.broadcasted_iota(jnp.int32, TILE, 1)

    def column(order, c):
        k = order * F + c
        return jnp.broadcast_to(gram[:, k:k + 1], TILE)

    def spread(value, row):
        return jnp.broadcast_to(value[row:row + 1], TILE)

    moments = [[column(order, c) for c in range(F)] for order in range(5)]
    columns = [[moments[2][c], moments[3][c]] for c in range(F)]
    columns += [[moments[3][c], moments[4][c]] for c in range(F)]
    rights = [[moments[1][c], moments[2][c]] for c in range(F)]
    for k in range(2 * F):
        half, row = k // F, k % F
        pivot = columns[k]
        inverse = 1.0 / spread(pivot[half], row)
        mine = sub == row
        for other in columns[k + 1:] + rights:
            r = spread(other[half], row) * inverse
            for h in range(2):
                value = other[h] - pivot[h] * r
                other[h] = jnp.where(mine, r, value) if h == half else value
    norms = jnp.zeros((1, 128), jnp.float32)
    for c in range(F):
        for h in range(2):
            coeff[c, h] = rights[c][h]
        fit = moments[1][c] * rights[c][0] + moments[2][c] * rights[c][1]
        left = jnp.where(sub == c, moments[0][c], 0.0) - fit
        norms = jnp.where(cell[0:1] == c, jnp.sum(left, axis=0, keepdims=True), norms)
    norm_ref[...] = jnp.sqrt(jnp.maximum(norms, 0.0))[:, :F]

    pair = 2
    outs = []
    for c0 in range(0, F, pair):
        weights = [[[spread(coeff[c, h], i) for i in range(F)] for h in range(2)] for c in range(c0, c0 + pair)]

        def step(x, _):
            for t in range(NY // 8):
                rows = slice(8 * t, 8 * t + 8)
                held = slice(TOP + 8 * t, TOP + 8 * t + 8)
                fields = [buf_b[:, x + 1, held], buf_a[:, x + 1, held]]
                for c in range(pair):
                    sums = [None, None]
                    for h in range(2):
                        for i in range(F):
                            term = weights[c][h][i] * fields[h][i]
                            sums[h] = term if sums[h] is None else sums[h] + term
                    buf_x[c0 + c, x, rows] = sums[0] + sums[1]
            return 0

        lax.fori_loop(0, NX, step, 0)
        out = pltpu.make_async_copy(buf_x.at[c0:c0 + pair], x_hbm.at[c0:c0 + pair], out_sem.at[c0 // pair])
        out.start()
        outs.append(out)
    for out in outs:
        out.wait()


def solution(mesh):
    gx, gy, gz = mesh.shape["gx"], mesh.shape["gy"], mesh.shape["gz"]
    f32 = jnp.float32
    dma = pltpu.SemaphoreType.DMA
    hbm = pl.BlockSpec(memory_space=pltpu.HBM)
    vmem = pl.BlockSpec(memory_space=pltpu.VMEM)
    block = (F, NX, NY, NZ)
    padded = (F, NX + 2, NY + 16, NZ)

    def body(right_side, shift):
        gram, fields, images = pl.pallas_call(
            functools.partial(exchange_kernel, gx, gy, gz),
            out_shape=(
                jax.ShapeDtypeStruct(TILE, f32),
                jax.ShapeDtypeStruct(padded, f32),
                jax.ShapeDtypeStruct(padded, f32),
            ),
            in_specs=[hbm, hbm],
            out_specs=(vmem, vmem, vmem),
            scratch_shapes=[
                pltpu.VMEM(padded, f32),
                pltpu.VMEM((NX, NY, NZ), f32),
                pltpu.VMEM(block, f32),
                pltpu.VMEM((2, 2, INNER, NZ), f32),
                pltpu.VMEM((2, 2, INNER, NZ), f32),
                pltpu.VMEM((2, 2, FACE, NZ), f32),
                pltpu.VMEM((2, 2, FACE, NZ), f32),
                pltpu.VMEM((2 * gz,) + TILE, f32),
                pltpu.VMEM((gx * gy // 2,) + TILE, f32),
                dma((4,)),
                dma((2, 2, GROUPS)),
                dma((2, 2, GROUPS)),
                dma((2, 2, 3)),
                dma((2, 2, 3)),
                dma((2, 2, 2)),
                dma((2, 2, 2)),
                dma((2,)),
                dma((2,)),
            ],
            compiler_params=pltpu.CompilerParams(
                collective_id=0, has_side_effects=True, vmem_limit_bytes=24 << 20
            ),
        )(*(pltpu.with_memory_space_constraint(a, pltpu.HBM) for a in (right_side, shift)))
        solved, norms = pl.pallas_call(
            combine_kernel,
            out_shape=(jax.ShapeDtypeStruct(block, f32), jax.ShapeDtypeStruct((1, F), f32)),
            in_specs=[vmem, vmem, vmem],
            out_specs=(hbm, vmem),
            scratch_shapes=[
                pltpu.VMEM(block, f32),
                pltpu.VMEM((F, 2) + TILE, f32),
                dma((F // 2,)),
            ],
            compiler_params=pltpu.CompilerParams(vmem_limit_bytes=16 << 20),
        )(gram, fields, images)
        return solved, norms.reshape(F)

    return jax.shard_map(
        body,
        mesh=mesh,
        in_specs=(P(None, "gx", "gy", "gz"), P("gx", "gy", "gz")),
        out_specs=(P(None, "gx", "gy", "gz"), P()),
        check_vma=False,
    )
```

time: 38.2 us -> 35.8 us (0.937)
  local copies, waits for them, and re-layouts: 2.12 us -> 0 us
    unnamed x4 -> x0, local copies, waits for them, and re-layouts: 2.12 us -> none
where the time goes in v2:
time: 35.8 us; the launch traced here: 35.7 us
  Pallas kernels  35.1 us (98%)
  between operations  0.64 us (2%)
    pallas_call x1, Pallas kernels, body(): pl.pallas_call(functools.partial(exchange_kernel, gx, gy, gz), out_shape=...  31.9 us
    pallas_call x1, Pallas kernels, body(): pl.pallas_call(combine_kernel, out_shape=(jax.ShapeDtypeStruct(block, f32...  3.2 us

profile of v2, /device:TPU:1, one launch (start us, length us, event | category | flops | bytes accessed | tf_op | source)
XLA Modules:
  0.0 35.7 jit_solution(5077167121535456290)
XLA Ops:
  0.6 31.9 %shard_map.41 = (f32[8,128]{1,0:T(8,128)S(1)}, f32[8,10,48,128]{3,2,1,0:T(8,128)S(1)}, f32[8,10,48,128]{3,2,1,0:T(8,128)S(1)}) custom-call(f32[8,8,32,128]{3,2,1,0:T(8,128)} %b_hbm.1, f32[8,32,128]{2,1,0:T(8,128)} %s_hbm.1), custom_call_target="tpu_custom_call" | custom-call | tf_op jit(solution)/shard_map/pallas_call | solution.py:407
  32.5 3.2 %shard_map.42 = (f32[8,8,32,128]{3,2,1,0:T(8,128)}, f32[1,8]{1,0:T(1,128)}) custom-call(f32[8,128]{1,0:T(8,128)S(1)} %get-tuple-element.7.gram_ref, f32[8,10,48,128]{3,2,1,0:T(8,128)S(1)} %get-tuple-element.8.buf_b, f32[8,10,48,128]{3,2,1,0:T(8,128)S(1)} %get-tuple-element.9.buf_a), custom_call_target="tpu_custom_call" | custom-call | tf_op jit(solution)/shard_map/pallas_call | solution.py:440

commit v3 on v2

--- a/solution.py
+++ b/solution.py
@@ -18,7 +18,7 @@
 
 
 def exchange_kernel(gx, gy, gz, b_hbm, s_hbm, gram_ref, buf_p, buf_q,
-                    buf_r, diag, side, inner_s, inner_r, face_s, face_r, part_z, part_p,
+                    buf_r, diag, y_halo, inner_s, inner_r, face_s, face_r, part_z, part_p,
                     load_sem, xs_sem, xr_sem, ys_sem, yr_sem, zs_sem, zr_sem, g_send, g_recv):
     ix, iy, iz = lax.axis_index("gx"), lax.axis_index("gy"), lax.axis_index("gz")
 
@@ -53,29 +53,23 @@
     zero_x = jnp.zeros((F, NY, NZ), jnp.float32)
     zero_y = jnp.zeros((F, NX, 1, NZ), jnp.float32)
     for turn, buf in enumerate((buf_p, buf_q)):
-        @pl.when(ix == 0)
-        def _():
-            buf[:, 0, ROWS] = zero_x
-
-        @pl.when(ix == gx - 1)
-        def _():
-            buf[:, NX + 1, ROWS] = zero_x
-
-        @pl.when(iy == 0)
-        def _():
-            buf[:, 1:NX + 1, TOP - 1:TOP] = zero_y
-
-        @pl.when(iy == gy - 1)
-        def _():
-            buf[:, 1:NX + 1, TOP + NY:TOP + NY + 1] = zero_y
-
-        for way, edge in enumerate((0, gz - 1)):
-            @pl.when(iz == edge)
+        buf[:, 1:NX + 1, TOP - 1:TOP] = zero_y
+        buf[:, 1:NX + 1, TOP + NY:TOP + NY + 1] = zero_y
+        for way in range(2):
+            @pl.when(ix == way * (gx - 1))
+            def _():
+                buf[:, way * (NX + 1), ROWS] = zero_x
+
+            @pl.when(iy == way * (gy - 1))
+            def _():
+                y_halo[turn, way] = zero_y
+
+            @pl.when(iz == way * (gz - 1))
             def _():
                 inner_r[turn, way] = jnp.zeros((INNER, NZ), jnp.float32)
                 face_r[turn, way] = jnp.zeros((FACE, NZ), jnp.float32)
 
-    bufs = (buf_p, buf_q)
+    bufs, both = (buf_p, buf_q), range(2)
     has = {
         "x": (ix > 0, ix < gx - 1),
         "y": (iy > 0, iy < gy - 1),
@@ -94,14 +88,14 @@
             device_id_type=MESH,
         )
 
-    planes = (slice(2, NX), slice(1, 2), slice(NX, NX + 1))
+    spans = ((2, NX), (1, 2), (NX, NX + 1))
 
     def y_copy(turn, way, part):
-        buf = bufs[turn]
-        src, dst = (TOP + NY - 1, TOP - 1) if way else (TOP, TOP + NY)
+        buf, (low, high) = bufs[turn], spans[part]
+        edge = TOP + NY - 1 if way else TOP
         return pltpu.make_async_remote_copy(
-            src_ref=buf.at[:, planes[part], src:src + 1],
-            dst_ref=buf.at[:, planes[part], dst:dst + 1],
+            src_ref=buf.at[:, low:high, edge:edge + 1],
+            dst_ref=y_halo.at[turn, 1 - way, :, low - 1:high - 1],
             send_sem=ys_sem.at[turn, way, part],
             recv_sem=yr_sem.at[turn, way, part],
             device_id=(ix, iy + 1 if way else iy - 1, iz),
@@ -152,7 +146,46 @@
             target[turn, 0, t:t + 1] = tile[0:1]
             target[turn, 1, t:t + 1] = tile[NZ - 1:NZ]
 
-    def unpack_z(turn, part):
+    lane = lax.broadcasted_iota(jnp.int32, (NY, NZ), 1)
+    first, last = lane == 0, lane == NZ - 1
+    edges = jnp.logical_or(first, last)
+
+    def apply(src, dst, f, x):
+        c = src[f, x, ROWS]
+        beside = src[f, x, TOP + 1:TOP + NY + 1] + src[f, x, TOP - 1:TOP + NY - 1]
+        for other in (x - 1, x + 1):
+            if 1 <= other <= NX:
+                beside = beside + src[f, other, ROWS]
+        beside = beside + jnp.where(last, 0.0, pltpu.roll(c, NZ - 1, 1))
+        beside = beside + jnp.where(first, 0.0, pltpu.roll(c, 1, 1))
+        dst[f, x, ROWS] = diag[x - 1] * c - beside
+
+    def inside(src, dst):
+        def step(f, _):
+            for x in range(1, NX + 1):
+                apply(src, dst, f, x)
+            return 0
+
+        lax.fori_loop(0, F, step, 0)
+
+    def take_x(src, dst, turn, group):
+        for way in both:
+            arrive("x", way, [x_copy(turn, way, group)])
+        for f in range(group * WIDE, (group + 1) * WIDE):
+            dst[f, 1, ROWS] -= src[f, 0, ROWS]
+            dst[f, NX, ROWS] -= src[f, NX + 1, ROWS]
+
+    def take_y(dst, turn, parts):
+        for way in both:
+            arrive("y", way, [y_copy(turn, way, part) for part in parts])
+        for part in parts:
+            low, high = spans[part]
+            for way, edge in enumerate((TOP, TOP + NY - 1)):
+                dst[:, low:high, edge:edge + 1] -= y_halo[turn, way, :, low - 1:high - 1]
+
+    def take_z(dst, turn, part):
+        for way in both:
+            arrive("z", way, [z_copy(turn, way, part)])
         source = (inner_r, face_r)[part]
         for t, pieces in enumerate(tiles[part]):
             low = jnp.broadcast_to(source[turn, 0, t:t + 1], (NZ // 2, NZ))
@@ -160,21 +193,8 @@
             tile = jnp.concatenate([low, high], axis=0).T.reshape(4, NY, NZ)
             at = 0
             for f, a, b in pieces:
-                side[f, a - 1:b - 1] = tile[at:at + b - a]
+                dst[f, a:b, ROWS] -= jnp.where(edges, tile[at:at + b - a], 0.0)
                 at += b - a
-
-    lane = lax.broadcasted_iota(jnp.int32, (NY, NZ), 1)
-    first, last = lane == 0, lane == NZ - 1
-
-    def apply(src, dst, f, x):
-        c = src[f, x, ROWS]
-        edge = side[f, x - 1]
-        beside = src[f, x + 1, ROWS] + src[f, x - 1, ROWS]
-        beside = beside + src[f, x, TOP + 1:TOP + NY + 1] + src[f, x, TOP - 1:TOP + NY - 1]
-        up = jnp.where(last, edge, pltpu.roll(c, NZ - 1, 1))
-        down = jnp.where(first, edge, pltpu.roll(c, 1, 1))
-        beside = beside + up + down
-        dst[f, x, ROWS] = (6.0 + diag[x - 1]) * c - beside
 
     def moment(left, right, low, high, sums):
         def step(x, sums):
@@ -225,25 +245,6 @@
             total = jnp.where(cell == order * F + c, jnp.sum(line, axis=1, keepdims=True), total)
         return total
 
-    def inner(src, dst):
-        def step(f, _):
-            for x in range(2, NX):
-                apply(src, dst, f, x)
-            return 0
-
-        lax.fori_loop(0, F, step, 0)
-
-    def outer(src, dst, turn, group):
-        for way in range(2):
-            arrive("x", way, [x_copy(turn, way, group)])
-        for f in range(group * WIDE, (group + 1) * WIDE):
-            for x in (1, NX):
-                apply(src, dst, f, x)
-        if turn == 0:
-            for way in range(2):
-                start("x", way, [x_copy(1, way, group)])
-
-    both = range(2)
     loads[0].wait()
     loads[1].wait()
     pl.semaphore_wait(barrier, len(greeted))
@@ -257,44 +258,48 @@
     for way in both:
         start("z", way, [z_copy(0, way, part) for part in both])
     loads[3].wait()
+    diag[...] = 6.0 + diag[...]
+    inside(buf_p, buf_q)
     zeroth = moment(buf_p, buf_p, 1, NX + 1, none)
     total = gather(0, zeroth, jnp.zeros(TILE, jnp.float32))
-    for way in both:
-        arrive("y", way, [y_copy(0, way, part) for part in range(3)])
-        arrive("z", way, [z_copy(0, way, part) for part in both])
+    take_y(buf_q, 0, range(3))
     for part in both:
-        unpack_z(0, part)
-
-    outer(buf_p, buf_q, 0, 0)
-    inner(buf_p, buf_q)
+        take_z(buf_q, 0, part)
+
+    def forward(group):
+        take_x(buf_p, buf_q, 0, group)
+        for way in both:
+            start("x", way, [x_copy(1, way, group)])
+
+    forward(0)
     for way in both:
         start("y", way, [y_copy(1, way, 0)])
     pack_z(1, 0)
     for way in both:
         start("z", way, [z_copy(1, way, 0)])
-    for group in range(1, GROUPS):
-        outer(buf_p, buf_q, 0, group)
+    forward(1)
+    first_sums = moment(buf_p, buf_q, 2, NX, none)
+    forward(2)
+    second_sums = moment(buf_q, buf_q, 2, NX, none)
+    for group in range(3, GROUPS):
+        forward(group)
     for way in both:
         start("y", way, [y_copy(1, way, part) for part in (1, 2)])
     pack_z(1, 1)
     for way in both:
         start("z", way, [z_copy(1, way, 1)])
-    total = gather(1, moment(buf_p, buf_q, 1, NX + 1, none), total)
-    total = gather(2, moment(buf_q, buf_q, 1, NX + 1, none), total)
-
-    for way in both:
-        arrive("y", way, [y_copy(1, way, 0)])
-        arrive("z", way, [z_copy(1, way, 0)])
-    unpack_z(1, 0)
-    inner(buf_q, buf_r)
+
+    inside(buf_q, buf_r)
+    total = gather(1, faces(buf_p, buf_q, first_sums), total)
+    total = gather(2, faces(buf_q, buf_q, second_sums), total)
+    take_y(buf_r, 1, (0,))
+    take_z(buf_r, 1, 0)
     third = moment(buf_q, buf_r, 2, NX, none)
     fourth = moment(buf_r, buf_r, 2, NX, none)
-    for way in both:
-        arrive("y", way, [y_copy(1, way, part) for part in (1, 2)])
-        arrive("z", way, [z_copy(1, way, 1)])
-    unpack_z(1, 1)
+    take_y(buf_r, 1, (1, 2))
+    take_z(buf_r, 1, 1)
     for group in range(GROUPS):
-        outer(buf_q, buf_r, 1, group)
+        take_x(buf_q, buf_r, 1, group)
     third = faces(buf_q, buf_r, third)
     fourth = faces(buf_r, buf_r, fourth)
     total = gather(3, third, total)
@@ -416,7 +421,7 @@
             scratch_shapes=[
                 pltpu.VMEM(padded, f32),
                 pltpu.VMEM((NX, NY, NZ), f32),
-                pltpu.VMEM(block, f32),
+                pltpu.VMEM((2, 2, F, NX, 1, NZ), f32),
                 pltpu.VMEM((2, 2, INNER, NZ), f32),
                 pltpu.VMEM((2, 2, INNER, NZ), f32),
                 pltpu.VMEM((2, 2, FACE, NZ), f32),

time: 35.8 us -> 33.7 us (0.941)
  Pallas kernels: 35.1 us -> 32.9 us
    pallas_call x1, Pallas kernels: 31.9 us -> 29.7 us  [body(): pl.pallas_call(functools.partial(exchange_kernel, gx, gy, gz), out_shape=...]
where the time goes in v3:
time: 33.7 us; the launch traced here: 33.6 us
  Pallas kernels  32.9 us (98%)
  between operations  0.64 us (2%)
    pallas_call x1, Pallas kernels, body(): pl.pallas_call(functools.partial(exchange_kernel, gx, gy, gz), out_shape=...  29.7 us
    pallas_call x1, Pallas kernels, body(): pl.pallas_call(combine_kernel, out_shape=(jax.ShapeDtypeStruct(block, f32...  3.2 us

profile of v3, /device:TPU:1, one launch (start us, length us, event | category | flops | bytes accessed | tf_op | source)
XLA Modules:
  0.0 33.6 jit_solution(8489359621102560177)
XLA Ops:
  0.6 29.7 %shard_map.41 = (f32[8,128]{1,0:T(8,128)S(1)}, f32[8,10,48,128]{3,2,1,0:T(8,128)S(1)}, f32[8,10,48,128]{3,2,1,0:T(8,128)S(1)}) custom-call(f32[8,8,32,128]{3,2,1,0:T(8,128)} %b_hbm.1, f32[8,32,128]{2,1,0:T(8,128)} %s_hbm.1), custom_call_target="tpu_custom_call" | custom-call | tf_op jit(solution)/shard_map/pallas_call | solution.py:412
  30.4 3.2 %shard_map.42 = (f32[8,8,32,128]{3,2,1,0:T(8,128)}, f32[1,8]{1,0:T(1,128)}) custom-call(f32[8,128]{1,0:T(8,128)S(1)} %get-tuple-element.7.gram_ref, f32[8,10,48,128]{3,2,1,0:T(8,128)S(1)} %get-tuple-element.8.buf_b, f32[8,10,48,128]{3,2,1,0:T(8,128)S(1)} %get-tuple-element.9.buf_a), custom_call_target="tpu_custom_call" | custom-call | tf_op jit(solution)/shard_map/pallas_call | solution.py:445

commit v4 on v3

--- a/solution.py
+++ b/solution.py
@@ -19,7 +19,7 @@
 
 def exchange_kernel(gx, gy, gz, b_hbm, s_hbm, gram_ref, buf_p, buf_q,
                     buf_r, diag, y_halo, inner_s, inner_r, face_s, face_r, part_z, part_p,
-                    load_sem, xs_sem, xr_sem, ys_sem, yr_sem, zs_sem, zr_sem, g_send, g_recv):
+                    load_sem, xs_sem, xr_sem, ys_sem, yr_sem, zs_sem, zr_sem, g_send, g_recv, heard):
     ix, iy, iz = lax.axis_index("gx"), lax.axis_index("gy"), lax.axis_index("gz")
 
     loads = [
@@ -42,13 +42,19 @@
     line = [(ix, y, zs[k]) for k in dict.fromkeys((1, gz - 1) + tuple(range(2, gz - 1))) for y in (iy, across)]
     line = [(ix, across, iz)] + line
     plane = [(xs[a], ys[b], iz) for a in range(gx) for b in range(chips_y) if a or b]
-    near = [(xs[k], iy, iz) for k in dict.fromkeys((1, gx - 1))] + [(ix, beyond, iz)]
-    rest = [(xs[a], ys[b], iz) for a in range(gx) for b in range(chips_y) if (a or b) and not (b == 0 and a in (1, gx - 1))]
-    greeted = near + line + rest
+    step_y = [ys[k] for k in dict.fromkeys((1, chips_y - 1))]
+    near = [(xs[k], iy, iz) for k in dict.fromkeys((1, gx - 1))] + [(ix, beyond, iz), (ix, across, iz)]
+    near += [(ix, iy, zs[k]) for k in dict.fromkeys((1, gz - 1))] + [(ix, y, iz) for y in step_y]
+    second = [(xs[2 % gx], iy, iz), (ix, ys[2 % chips_y], iz)] if gx > 2 and chips_y > 2 else []
+    second += [(ix, iy, zs[k]) for k in dict.fromkeys((2, gz - 2))] if gz > 3 else []
 
     barrier = pltpu.get_barrier_semaphore()
-    for device in greeted:
+    for device in near:
         pl.semaphore_signal(barrier, inc=1, device_id=device, device_id_type=MESH)
+
+    def tell(stage, devices):
+        for device in devices:
+            pl.semaphore_signal(heard.at[stage], inc=1, device_id=device, device_id_type=MESH)
 
     zero_x = jnp.zeros((F, NY, NZ), jnp.float32)
     zero_y = jnp.zeros((F, NX, 1, NZ), jnp.float32)
@@ -247,9 +253,10 @@
 
     loads[0].wait()
     loads[1].wait()
-    pl.semaphore_wait(barrier, len(greeted))
+    pl.semaphore_wait(barrier, len(near))
     for way in both:
         start("x", way, [x_copy(0, way, group) for group in range(GROUPS)])
+    tell(0, near)
     loads[2].wait()
     for way in both:
         start("y", way, [y_copy(0, way, part) for part in range(3)])
@@ -262,6 +269,8 @@
     inside(buf_p, buf_q)
     zeroth = moment(buf_p, buf_p, 1, NX + 1, none)
     total = gather(0, zeroth, jnp.zeros(TILE, jnp.float32))
+    pl.semaphore_wait(heard.at[0], len(near))
+    tell(1, second)
     take_y(buf_q, 0, range(3))
     for part in both:
         take_z(buf_q, 0, part)
@@ -288,6 +297,10 @@
     pack_z(1, 1)
     for way in both:
         start("z", way, [z_copy(1, way, 1)])
+
+    if second:
+        pl.semaphore_wait(heard.at[1], len(second))
+    tell(2, [(ix, across, iz)])
 
     inside(buf_q, buf_r)
     total = gather(1, faces(buf_p, buf_q, first_sums), total)
@@ -304,6 +317,8 @@
     fourth = faces(buf_r, buf_r, fourth)
     total = gather(3, third, total)
     total = gather(4, fourth, total)
+
+    pl.semaphore_wait(heard.at[2], 1)
 
     def spread(stage, parts, mine, devices, total):
         slots = len(devices) + 1
@@ -437,6 +452,7 @@
                 dma((2, 2, 2)),
                 dma((2,)),
                 dma((2,)),
+                pltpu.SemaphoreType.REGULAR((3,)),
             ],
             compiler_params=pltpu.CompilerParams(
                 collective_id=0, has_side_effects=True, vmem_limit_bytes=24 << 20

time: 33.7 us -> 32.1 us (0.953)
  Pallas kernels: 32.9 us -> 31.3 us
    pallas_call x1, Pallas kernels: 29.7 us -> 28.1 us  [body(): pl.pallas_call(functools.partial(exchange_kernel, gx, gy, gz), out_shape=...]
where the time goes in v4:
time: 32.1 us; the launch traced here: 32 us
  Pallas kernels  31.3 us (98%)
  between operations  0.64 us (2%)
    pallas_call x1, Pallas kernels, body(): pl.pallas_call(functools.partial(exchange_kernel, gx, gy, gz), out_shape=...  28.1 us
    pallas_call x1, Pallas kernels, body(): pl.pallas_call(combine_kernel, out_shape=(jax.ShapeDtypeStruct(block, f32...  3.2 us

profile of v4, /device:TPU:1, one launch (start us, length us, event | category | flops | bytes accessed | tf_op | source)
XLA Modules:
  0.0 32.0 jit_solution(8753384427640646384)
XLA Ops:
  0.6 28.1 %shard_map.41 = (f32[8,128]{1,0:T(8,128)S(1)}, f32[8,10,48,128]{3,2,1,0:T(8,128)S(1)}, f32[8,10,48,128]{3,2,1,0:T(8,128)S(1)}) custom-call(f32[8,8,32,128]{3,2,1,0:T(8,128)} %b_hbm.1, f32[8,32,128]{2,1,0:T(8,128)} %s_hbm.1), custom_call_target="tpu_custom_call" | custom-call | tf_op jit(solution)/shard_map/pallas_call | solution.py:427
  28.8 3.2 %shard_map.42 = (f32[8,8,32,128]{3,2,1,0:T(8,128)}, f32[1,8]{1,0:T(1,128)}) custom-call(f32[8,128]{1,0:T(8,128)S(1)} %get-tuple-element.7.gram_ref, f32[8,10,48,128]{3,2,1,0:T(8,128)S(1)} %get-tuple-element.8.buf_b, f32[8,10,48,128]{3,2,1,0:T(8,128)S(1)} %get-tuple-element.9.buf_a), custom_call_target="tpu_custom_call" | custom-call | tf_op jit(solution)/shard_map/pallas_call | solution.py:461

commit v5 on v4

--- a/solution.py
+++ b/solution.py
@@ -18,7 +18,7 @@
 
 
 def exchange_kernel(gx, gy, gz, b_hbm, s_hbm, gram_ref, buf_p, buf_q,
-                    buf_r, diag, y_halo, inner_s, inner_r, face_s, face_r, part_z, part_p,
+                    buf_r, diag, y_halo, inner_s, inner_r, face_s, face_r, part_e, part_l, part_p,
                     load_sem, xs_sem, xr_sem, ys_sem, yr_sem, zs_sem, zr_sem, g_send, g_recv, heard):
     ix, iy, iz = lax.axis_index("gx"), lax.axis_index("gy"), lax.axis_index("gz")
 
@@ -42,7 +42,7 @@
     line = [(ix, y, zs[k]) for k in dict.fromkeys((1, gz - 1) + tuple(range(2, gz - 1))) for y in (iy, across)]
     line = [(ix, across, iz)] + line
     plane = [(xs[a], ys[b], iz) for a in range(gx) for b in range(chips_y) if a or b]
-    step_y = [ys[k] for k in dict.fromkeys((1, chips_y - 1))]
+    step_y = [ys[k] for k in dict.fromkeys((1, chips_y - 1)) if k % chips_y]
     near = [(xs[k], iy, iz) for k in dict.fromkeys((1, gx - 1))] + [(ix, beyond, iz), (ix, across, iz)]
     near += [(ix, iy, zs[k]) for k in dict.fromkeys((1, gz - 1))] + [(ix, y, iz) for y in step_y]
     second = [(xs[2 % gx], iy, iz), (ix, ys[2 % chips_y], iz)] if gx > 2 and chips_y > 2 else []
@@ -245,11 +245,37 @@
             width *= 2
         return parts[0]
 
-    def gather(order, sums, total):
+    place = lax.rem(cell, 2 * F)
+    own = sub == lax.rem(F - lax.div(cell, 2 * F), F)
+
+    def gather(k, sums, total):
         for c in range(F):
             line = fold([sums[min(i, c)][max(i, c) - min(i, c)] for i in range(F)])
-            total = jnp.where(cell == order * F + c, jnp.sum(line, axis=1, keepdims=True), total)
+            total = jnp.where(place == k * F + c, jnp.sum(line, axis=1, keepdims=True), total)
         return total
+
+    def as_row(total):
+        return jnp.sum(jnp.where(own, total, 0.0), axis=0, keepdims=True)
+
+    def copy_part(stage, src, dst, device):
+        return pltpu.make_async_remote_copy(
+            src_ref=src, dst_ref=dst,
+            send_sem=g_send.at[stage], recv_sem=g_recv.at[stage],
+            device_id=device, device_id_type=MESH)
+
+    def spread(stage, parts, mine, devices, rows):
+        for k, value in enumerate(rows):
+            parts[mine, k:k + 1] = value
+        for device in devices:
+            copy_part(stage, parts.at[mine], parts.at[mine], device).start()
+        count = len(devices)
+        return copy_part(stage, parts.at[0:count], parts.at[0:count], devices[0])
+
+    def added(parts, count):
+        sums = [parts[k] for k in range(count)]
+        while len(sums) > 1:
+            sums = [sums[k] + sums[k + 1] for k in range(0, len(sums), 2)]
+        return sums[0]
 
     loads[0].wait()
     loads[1].wait()
@@ -268,7 +294,8 @@
     diag[...] = 6.0 + diag[...]
     inside(buf_p, buf_q)
     zeroth = moment(buf_p, buf_p, 1, NX + 1, none)
-    total = gather(0, zeroth, jnp.zeros(TILE, jnp.float32))
+    blank = jnp.zeros(TILE, jnp.float32)
+    row_zero = as_row(gather(0, zeroth, blank))
     pl.semaphore_wait(heard.at[0], len(near))
     tell(1, second)
     take_y(buf_q, 0, range(3))
@@ -303,8 +330,12 @@
     tell(2, [(ix, across, iz)])
 
     inside(buf_q, buf_r)
-    total = gather(1, faces(buf_p, buf_q, first_sums), total)
-    total = gather(2, faces(buf_q, buf_q, second_sums), total)
+    total = gather(0, faces(buf_p, buf_q, first_sums), blank)
+    total = gather(1, faces(buf_q, buf_q, second_sums), total)
+    row_one = as_row(total)
+    pl.semaphore_wait(heard.at[2], 1)
+    in_line = 2 * iz + core
+    early_done = spread(0, part_e, in_line, line, (row_zero, row_one))
     take_y(buf_r, 1, (0,))
     take_z(buf_r, 1, 0)
     third = moment(buf_q, buf_r, 2, NX, none)
@@ -315,35 +346,20 @@
         take_x(buf_q, buf_r, 1, group)
     third = faces(buf_q, buf_r, third)
     fourth = faces(buf_r, buf_r, fourth)
-    total = gather(3, third, total)
-    total = gather(4, fourth, total)
-
-    pl.semaphore_wait(heard.at[2], 1)
-
-    def spread(stage, parts, mine, devices, total):
-        slots = len(devices) + 1
-        parts[mine] = total
-
-        def copy(src, dst, device):
-            return pltpu.make_async_remote_copy(
-                src_ref=src, dst_ref=dst,
-                send_sem=g_send.at[stage], recv_sem=g_recv.at[stage],
-                device_id=device, device_id_type=MESH)
-
-        for device in devices:
-            copy(parts.at[mine], parts.at[mine], device).start()
-        every = copy(parts.at[0:slots - 1], parts.at[0:slots - 1], devices[0])
-        every.wait_recv()
-        sums = [parts[k] for k in range(slots)]
-        while len(sums) > 1:
-            sums = [sums[k] + sums[k + 1] for k in range(0, len(sums), 2)]
-        return sums[0], every
-
-    total, lines_done = spread(0, part_z, 2 * iz + core, line, total)
-    total, planes_done = spread(1, part_p, ix * chips_y + lax.div(row, 2), plane, total)
-    gram_ref[...] = total
-
-    lines_done.wait_send()
+    row_two = as_row(gather(1, fourth, gather(0, third, blank)))
+
+    late_done = spread(1, part_l, in_line, line, (row_two,))
+    early_done.wait_recv()
+    early = added(part_e, len(line) + 1)
+    late_done.wait_recv()
+    late = added(part_l, len(line) + 1)
+    chip = ix * chips_y + lax.div(row, 2)
+    planes_done = spread(2, part_p, chip, plane, (early[0:1], early[1:2], late))
+    planes_done.wait_recv()
+    gram_ref[...] = added(part_p, len(plane) + 1)
+
+    early_done.wait_send()
+    late_done.wait_send()
     planes_done.wait_send()
     for turn in both:
         for way in both:
@@ -353,13 +369,16 @@
 
 
 def combine_kernel(gram_ref, buf_b, buf_a, x_hbm, norm_ref, buf_x, coeff, out_sem):
-    gram = gram_ref[...]
+    turned = [
+        pltpu.roll(jnp.broadcast_to(gram_ref[k:k + 1], TILE), 0, 1, stride=2 * F, stride_axis=0) for k in range(3)
+    ]
     sub = lax.broadcasted_iota(jnp.int32, TILE, 0)
     cell = lax.broadcasted_iota(jnp.int32, TILE, 1)
 
     def column(order, c):
-        k = order * F + c
-        return jnp.broadcast_to(gram[:, k:k + 1], TILE)
+        k, half = ((0, 0), (1, 0), (1, 1), (2, 0), (2, 1))[order]
+        at = half * F + c
+        return jnp.broadcast_to(turned[k][:, at:at + 1], TILE)
 
     def spread(value, row):
         return jnp.broadcast_to(value[row:row + 1], TILE)
@@ -427,7 +446,7 @@
         gram, fields, images = pl.pallas_call(
             functools.partial(exchange_kernel, gx, gy, gz),
             out_shape=(
-                jax.ShapeDtypeStruct(TILE, f32),
+                jax.ShapeDtypeStruct((3, NZ), f32),
                 jax.ShapeDtypeStruct(padded, f32),
                 jax.ShapeDtypeStruct(padded, f32),
             ),
@@ -441,8 +460,9 @@
                 pltpu.VMEM((2, 2, INNER, NZ), f32),
                 pltpu.VMEM((2, 2, FACE, NZ), f32),
                 pltpu.VMEM((2, 2, FACE, NZ), f32),
-                pltpu.VMEM((2 * gz,) + TILE, f32),
-                pltpu.VMEM((gx * gy // 2,) + TILE, f32),
+                pltpu.VMEM((2 * gz, 2, NZ), f32),
+                pltpu.VMEM((2 * gz, 1, NZ), f32),
+                pltpu.VMEM((gx * gy // 2, 3, NZ), f32),
                 dma((4,)),
                 dma((2, 2, GROUPS)),
                 dma((2, 2, GROUPS)),
@@ -450,8 +470,8 @@
                 dma((2, 2, 3)),
                 dma((2, 2, 2)),
                 dma((2, 2, 2)),
-                dma((2,)),
-                dma((2,)),
+                dma((3,)),
+                dma((3,)),
                 pltpu.SemaphoreType.REGULAR((3,)),
             ],
             compiler_params=pltpu.CompilerParams(

time: 32.1 us -> 31.4 us (0.978)
  Pallas kernels: 31.3 us -> 30.7 us
    pallas_call x1, Pallas kernels: 28.1 us -> 27.4 us  [body(): pl.pallas_call(functools.partial(exchange_kernel, gx, gy, gz), out_shape=...]
where the time goes in v5:
time: 31.4 us; the launch traced here: 31.3 us
  Pallas kernels  30.7 us (98%)
  between operations  0.64 us (2%)
    pallas_call x1, Pallas kernels, body(): pl.pallas_call(functools.partial(exchange_kernel, gx, gy, gz), out_shape=...  27.4 us
    pallas_call x1, Pallas kernels, body(): pl.pallas_call(combine_kernel, out_shape=(jax.ShapeDtypeStruct(block, f32...  3.3 us

profile of v5, /device:TPU:1, one launch (start us, length us, event | category | flops | bytes accessed | tf_op | source)
XLA Modules:
  0.0 31.3 jit_solution(17690738684212932726)
XLA Ops:
  0.6 27.4 %shard_map.41 = (f32[3,128]{1,0:T(4,128)S(1)}, f32[8,10,48,128]{3,2,1,0:T(8,128)S(1)}, f32[8,10,48,128]{3,2,1,0:T(8,128)S(1)}) custom-call(f32[8,8,32,128]{3,2,1,0:T(8,128)} %b_hbm.1, f32[8,32,128]{2,1,0:T(8,128)} %s_hbm.1), custom_call_target="tpu_custom_call" | custom-call | tf_op jit(solution)/shard_map/pallas_call | solution.py:446
  28.0 3.3 %shard_map.42 = (f32[8,8,32,128]{3,2,1,0:T(8,128)}, f32[1,8]{1,0:T(1,128)}) custom-call(f32[3,128]{1,0:T(4,128)S(1)} %get-tuple-element.7.gram_ref, f32[8,10,48,128]{3,2,1,0:T(8,128)S(1)} %get-tuple-element.8.buf_b, f32[8,10,48,128]{3,2,1,0:T(8,128)S(1)} %get-tuple-element.9.buf_a), custom_call_target="tpu_custom_call" | custom-call | tf_op jit(solution)/shard_map/pallas_call | solution.py:481

commit v6 on v5

--- a/solution.py
+++ b/solution.py
@@ -39,9 +39,13 @@
     zs = [iz] + [lax.rem(iz + k, gz) for k in range(1, gz)]
     across = row + 1 - core
     beyond = lax.rem(iy + gy - 1 + 2 * core, gy)
-    line = [(ix, y, zs[k]) for k in dict.fromkeys((1, gz - 1) + tuple(range(2, gz - 1))) for y in (iy, across)]
-    line = [(ix, across, iz)] + line
-    plane = [(xs[a], ys[b], iz) for a in range(gx) for b in range(chips_y) if a or b]
+    def hops(k, n):
+        return min(k, n - k)
+
+    line = [(ix, y, zs[k]) for k in sorted(range(1, gz), key=lambda k: -hops(k, gz)) for y in (across, iy)]
+    line += [(ix, across, iz)]
+    steps = sorted(((a, b) for a in range(gx) for b in range(chips_y)), key=lambda p: -hops(p[0], gx) - hops(p[1], chips_y))
+    plane = [(xs[a], ys[b], iz) for a, b in steps if a or b]
     step_y = [ys[k] for k in dict.fromkeys((1, chips_y - 1)) if k % chips_y]
     near = [(xs[k], iy, iz) for k in dict.fromkeys((1, gx - 1))] + [(ix, beyond, iz), (ix, across, iz)]
     near += [(ix, iy, zs[k]) for k in dict.fromkeys((1, gz - 1))] + [(ix, y, iz) for y in step_y]
@@ -156,23 +160,29 @@
     first, last = lane == 0, lane == NZ - 1
     edges = jnp.logical_or(first, last)
 
-    def apply(src, dst, f, x):
-        c = src[f, x, ROWS]
-        beside = src[f, x, TOP + 1:TOP + NY + 1] + src[f, x, TOP - 1:TOP + NY - 1]
-        for other in (x - 1, x + 1):
-            if 1 <= other <= NX:
-                beside = beside + src[f, other, ROWS]
-        beside = beside + jnp.where(last, 0.0, pltpu.roll(c, NZ - 1, 1))
-        beside = beside + jnp.where(first, 0.0, pltpu.roll(c, 1, 1))
-        dst[f, x, ROWS] = diag[x - 1] * c - beside
-
-    def inside(src, dst):
-        def step(f, _):
-            for x in range(1, NX + 1):
-                apply(src, dst, f, x)
-            return 0
-
-        lax.fori_loop(0, F, step, 0)
+    def dots(left, right, x, sums):
+        for t in range(NY // 8):
+            rows = slice(TOP + 8 * t, TOP + 8 * t + 8)
+            u = left[:, x, rows]
+            v = u if right is left else right[:, x, rows]
+            sums = tuple(sums[i] + u[i:i + 1] * v[i:] for i in range(F))
+        return sums
+
+    def inside(src, dst, left, right, sums):
+        def step(x, sums):
+            for f in range(F):
+                c = src[f, x, ROWS]
+                beside = src[f, x, TOP + 1:TOP + NY + 1] + src[f, x, TOP - 1:TOP + NY - 1]
+                for other in (x - 1, x + 1):
+                    if not isinstance(x, int) or 1 <= other <= NX:
+                        beside = beside + src[f, other, ROWS]
+                beside = beside + jnp.where(last, 0.0, pltpu.roll(c, NZ - 1, 1))
+                beside = beside + jnp.where(first, 0.0, pltpu.roll(c, 1, 1))
+                dst[f, x, ROWS] = diag[x - 1] * c - beside
+            return dots(left, right, x, sums)
+
+        sums = lax.fori_loop(2, NX, step, step(1, sums))
+        return step(NX, sums)
 
     def take_x(src, dst, turn, group):
         for way in both:
@@ -203,27 +213,10 @@
                 at += b - a
 
     def moment(left, right, low, high, sums):
-        def step(x, sums):
-            for t in range(NY // 8):
-                rows = slice(TOP + 8 * t, TOP + 8 * t + 8)
-                u = left[:, x, rows]
-                v = u if right is left else right[:, x, rows]
-                sums = tuple(sums[i] + u[i:i + 1] * v[i:] for i in range(F))
-            return sums
-
-        return lax.fori_loop(low, high, step, sums)
+        return lax.fori_loop(low, high, lambda x, sums: dots(left, right, x, sums), sums)
 
     def faces(left, right, sums):
-        def step(k, sums):
-            x = 1 + (NX - 1) * k
-            for t in range(NY // 8):
-                rows = slice(TOP + 8 * t, TOP + 8 * t + 8)
-                u = left[:, x, rows]
-                v = u if right is left else right[:, x, rows]
-                sums = tuple(sums[i] + u[i:i + 1] * v[i:] for i in range(F))
-            return sums
-
-        return lax.fori_loop(0, 2, step, sums)
+        return lax.fori_loop(0, 2, lambda k, sums: dots(left, right, 1 + (NX - 1) * k, sums), sums)
 
     none = tuple(jnp.zeros((F - i,) + TILE, jnp.float32) for i in range(F))
 
@@ -292,8 +285,7 @@
         start("z", way, [z_copy(0, way, part) for part in both])
     loads[3].wait()
     diag[...] = 6.0 + diag[...]
-    inside(buf_p, buf_q)
-    zeroth = moment(buf_p, buf_p, 1, NX + 1, none)
+    zeroth = inside(buf_p, buf_q, buf_p, buf_p, none)
     blank = jnp.zeros(TILE, jnp.float32)
     row_zero = as_row(gather(0, zeroth, blank))
     pl.semaphore_wait(heard.at[0], len(near))
@@ -314,9 +306,8 @@
     for way in both:
         start("z", way, [z_copy(1, way, 0)])
     forward(1)
-    first_sums = moment(buf_p, buf_q, 2, NX, none)
+    second_sums = moment(buf_q, buf_q, 2, NX, none)
     forward(2)
-    second_sums = moment(buf_q, buf_q, 2, NX, none)
     for group in range(3, GROUPS):
         forward(group)
     for way in both:
@@ -329,8 +320,7 @@
         pl.semaphore_wait(heard.at[1], len(second))
     tell(2, [(ix, across, iz)])
 
-    inside(buf_q, buf_r)
-    total = gather(0, faces(buf_p, buf_q, first_sums), blank)
+    total = gather(0, inside(buf_q, buf_r, buf_p, buf_q, none), blank)
     total = gather(1, faces(buf_q, buf_q, second_sums), total)
     row_one = as_row(total)
     pl.semaphore_wait(heard.at[2], 1)

time: 31.4 us -> 31.3 us (level)
  no operation moved by 1% of the time
where the time goes in v6:
time: 31.3 us; the launch traced here: 31.2 us
  Pallas kernels  30.5 us (97%)
  between operations  0.64 us (2%)
    pallas_call x1, Pallas kernels, body(): pl.pallas_call(functools.partial(exchange_kernel, gx, gy, gz), out_shape=...  27.2 us
    pallas_call x1, Pallas kernels, body(): pl.pallas_call(combine_kernel, out_shape=(jax.ShapeDtypeStruct(block, f32...  3.3 us

profile of v6, /device:TPU:1, one launch (start us, length us, event | category | flops | bytes accessed | tf_op | source)
XLA Modules:
  0.0 31.2 jit_solution(14545615694545229934)
XLA Ops:
  0.6 27.2 %shard_map.41 = (f32[3,128]{1,0:T(4,128)S(1)}, f32[8,10,48,128]{3,2,1,0:T(8,128)S(1)}, f32[8,10,48,128]{3,2,1,0:T(8,128)S(1)}) custom-call(f32[8,8,32,128]{3,2,1,0:T(8,128)} %b_hbm.1, f32[8,32,128]{2,1,0:T(8,128)} %s_hbm.1), custom_call_target="tpu_custom_call" | custom-call | tf_op jit(solution)/shard_map/pallas_call | solution.py:436
  27.9 3.3 %shard_map.42 = (f32[8,8,32,128]{3,2,1,0:T(8,128)}, f32[1,8]{1,0:T(1,128)}) custom-call(f32[3,128]{1,0:T(4,128)S(1)} %get-tuple-element.7.gram_ref, f32[8,10,48,128]{3,2,1,0:T(8,128)S(1)} %get-tuple-element.8.buf_b, f32[8,10,48,128]{3,2,1,0:T(8,128)S(1)} %get-tuple-element.9.buf_a), custom_call_target="tpu_custom_call" | custom-call | tf_op jit(solution)/shard_map/pallas_call | solution.py:471

commit v7 on v6

--- a/solution.py
+++ b/solution.py
@@ -396,31 +396,27 @@
         norms = jnp.where(cell[0:1] == c, jnp.sum(left, axis=0, keepdims=True), norms)
     norm_ref[...] = jnp.sqrt(jnp.maximum(norms, 0.0))[:, :F]
 
-    pair = 2
-    outs = []
-    for c0 in range(0, F, pair):
-        weights = [[[spread(coeff[c, h], i) for i in range(F)] for h in range(2)] for c in range(c0, c0 + pair)]
-
-        def step(x, _):
-            for t in range(NY // 8):
-                rows = slice(8 * t, 8 * t + 8)
-                held = slice(TOP + 8 * t, TOP + 8 * t + 8)
-                fields = [buf_b[:, x + 1, held], buf_a[:, x + 1, held]]
-                for c in range(pair):
-                    sums = [None, None]
-                    for h in range(2):
-                        for i in range(F):
-                            term = weights[c][h][i] * fields[h][i]
-                            sums[h] = term if sums[h] is None else sums[h] + term
-                    buf_x[c0 + c, x, rows] = sums[0] + sums[1]
-            return 0
-
-        lax.fori_loop(0, NX, step, 0)
-        out = pltpu.make_async_copy(buf_x.at[c0:c0 + pair], x_hbm.at[c0:c0 + pair], out_sem.at[c0 // pair])
-        out.start()
-        outs.append(out)
-    for out in outs:
-        out.wait()
+    def out(x):
+        return pltpu.make_async_copy(buf_x.at[:, x], x_hbm.at[:, x], out_sem.at[x])
+
+    def step(x, _):
+        for t in range(NY // 8):
+            rows = slice(8 * t, 8 * t + 8)
+            held = slice(TOP + 8 * t, TOP + 8 * t + 8)
+            fields = [buf_b[:, x + 1, held], buf_a[:, x + 1, held]]
+            for c in range(F):
+                sums = [None, None]
+                for h in range(2):
+                    for i in range(F):
+                        term = jnp.broadcast_to(coeff[c, h, i:i + 1], TILE) * fields[h][i]
+                        sums[h] = term if sums[h] is None else sums[h] + term
+                buf_x[c, x, rows] = sums[0] + sums[1]
+        out(x).start()
+        return 0
+
+    lax.fori_loop(0, NX, step, 0)
+    for x in range(NX):
+        out(x).wait()
 
 
 def solution(mesh):
@@ -476,7 +472,7 @@
             scratch_shapes=[
                 pltpu.VMEM(block, f32),
                 pltpu.VMEM((F, 2) + TILE, f32),
-                dma((F // 2,)),
+                dma((NX,)),
             ],
             compiler_params=pltpu.CompilerParams(vmem_limit_bytes=16 << 20),
         )(gram, fields, images)

time: 31.3 us -> 31 us (level)
  no operation moved by 1% of the time
where the time goes in v7:
time: 31 us; the launch traced here: 30.9 us
  Pallas kernels  30.2 us (97%)
  between operations  0.64 us (2%)
    pallas_call x1, Pallas kernels, body(): pl.pallas_call(functools.partial(exchange_kernel, gx, gy, gz), out_shape=...  27.2 us
    pallas_call x1, Pallas kernels, body(): pl.pallas_call(combine_kernel, out_shape=(jax.ShapeDtypeStruct(block, f32...  3 us

profile of v7, /device:TPU:1, one launch (start us, length us, event | category | flops | bytes accessed | tf_op | source)
XLA Modules:
  0.0 30.9 jit_solution(12728220219387694019)
XLA Ops:
  0.6 27.2 %shard_map.41 = (f32[3,128]{1,0:T(4,128)S(1)}, f32[8,10,48,128]{3,2,1,0:T(8,128)S(1)}, f32[8,10,48,128]{3,2,1,0:T(8,128)S(1)}) custom-call(f32[8,8,32,128]{3,2,1,0:T(8,128)} %b_hbm.1, f32[8,32,128]{2,1,0:T(8,128)} %s_hbm.1), custom_call_target="tpu_custom_call" | custom-call | tf_op jit(solution)/shard_map/pallas_call | solution.py:432
  27.9 3.0 %shard_map.42 = (f32[8,8,32,128]{3,2,1,0:T(8,128)}, f32[1,8]{1,0:T(1,128)}) custom-call(f32[3,128]{1,0:T(4,128)S(1)} %get-tuple-element.7.gram_ref, f32[8,10,48,128]{3,2,1,0:T(8,128)S(1)} %get-tuple-element.8.buf_b, f32[8,10,48,128]{3,2,1,0:T(8,128)S(1)} %get-tuple-element.9.buf_a), custom_call_target="tpu_custom_call" | custom-call | tf_op jit(solution)/shard_map/pallas_call | solution.py:467

commit v8 on v7

--- a/solution.py
+++ b/solution.py
@@ -11,8 +11,8 @@
 F, NX, NY, NZ = 8, 8, 32, 128
 TOP = 8
 ROWS = slice(TOP, TOP + NY)
-GROUPS = 4
-WIDE = F // GROUPS
+CUTS = (0, 4, 7, 8)
+GROUPS = len(CUTS) - 1
 INNER, FACE = 12, 4
 TILE = (8, 128)
 
@@ -87,7 +87,7 @@
     }
 
     def x_copy(turn, way, group):
-        fields = slice(group * WIDE, (group + 1) * WIDE)
+        fields = slice(CUTS[group], CUTS[group + 1])
         buf = bufs[turn]
         return pltpu.make_async_remote_copy(
             src_ref=buf.at[fields, NX if way else 1, ROWS],
@@ -98,7 +98,8 @@
             device_id_type=MESH,
         )
 
-    spans = ((2, NX), (1, 2), (NX, NX + 1))
+    spans = ((2, NX), (1, 2), (NX, NX + 1), (1, NX + 1))
+    y_parts = ((3,), (0, 1, 2))
 
     def y_copy(turn, way, part):
         buf, (low, high) = bufs[turn], spans[part]
@@ -184,10 +185,25 @@
         sums = lax.fori_loop(2, NX, step, step(1, sums))
         return step(NX, sums)
 
+    def alone(src, dst):
+        def step(f, _):
+            for x in range(1, NX + 1):
+                c = src[f, x, ROWS]
+                beside = src[f, x, TOP + 1:TOP + NY + 1] + src[f, x, TOP - 1:TOP + NY - 1]
+                for other in (x - 1, x + 1):
+                    if 1 <= other <= NX:
+                        beside = beside + src[f, other, ROWS]
+                beside = beside + jnp.where(last, 0.0, pltpu.roll(c, NZ - 1, 1))
+                beside = beside + jnp.where(first, 0.0, pltpu.roll(c, 1, 1))
+                dst[f, x, ROWS] = diag[x - 1] * c - beside
+            return 0
+
+        lax.fori_loop(0, F, step, 0)
+
     def take_x(src, dst, turn, group):
         for way in both:
             arrive("x", way, [x_copy(turn, way, group)])
-        for f in range(group * WIDE, (group + 1) * WIDE):
+        for f in range(CUTS[group], CUTS[group + 1]):
             dst[f, 1, ROWS] -= src[f, 0, ROWS]
             dst[f, NX, ROWS] -= src[f, NX + 1, ROWS]
 
@@ -278,7 +294,7 @@
     tell(0, near)
     loads[2].wait()
     for way in both:
-        start("y", way, [y_copy(0, way, part) for part in range(3)])
+        start("y", way, [y_copy(0, way, part) for part in y_parts[0]])
     for part in both:
         pack_z(0, part)
     for way in both:
@@ -290,7 +306,7 @@
     row_zero = as_row(gather(0, zeroth, blank))
     pl.semaphore_wait(heard.at[0], len(near))
     tell(1, second)
-    take_y(buf_q, 0, range(3))
+    take_y(buf_q, 0, y_parts[0])
     for part in both:
         take_z(buf_q, 0, part)
 
@@ -320,7 +336,8 @@
         pl.semaphore_wait(heard.at[1], len(second))
     tell(2, [(ix, across, iz)])
 
-    total = gather(0, inside(buf_q, buf_r, buf_p, buf_q, none), blank)
+    alone(buf_q, buf_r)
+    total = gather(0, moment(buf_p, buf_q, 1, NX + 1, none), blank)
     total = gather(1, faces(buf_q, buf_q, second_sums), total)
     row_one = as_row(total)
     pl.semaphore_wait(heard.at[2], 1)
@@ -354,7 +371,7 @@
     for turn in both:
         for way in both:
             sent("x", way, [x_copy(turn, way, group) for group in range(GROUPS)])
-            sent("y", way, [y_copy(turn, way, part) for part in range(3)])
+            sent("y", way, [y_copy(turn, way, part) for part in y_parts[turn]])
             sent("z", way, [z_copy(turn, way, part) for part in both])
 
 
@@ -452,8 +469,8 @@
                 dma((4,)),
                 dma((2, 2, GROUPS)),
                 dma((2, 2, GROUPS)),
-                dma((2, 2, 3)),
-                dma((2, 2, 3)),
+                dma((2, 2, 4)),
+                dma((2, 2, 4)),
                 dma((2, 2, 2)),
                 dma((2, 2, 2)),
                 dma((3,)),

time: 31 us -> 31 us (level)
  no operation moved by 1% of the time
where the time goes in v8:
time: 31 us; the launch traced here: 30.9 us
  Pallas kernels  30.2 us (97%)
  between operations  0.64 us (2%)
    pallas_call x1, Pallas kernels, body(): pl.pallas_call(functools.partial(exchange_kernel, gx, gy, gz), out_shape=...  27.2 us
    pallas_call x1, Pallas kernels, body(): pl.pallas_call(combine_kernel, out_shape=(jax.ShapeDtypeStruct(block, f32...  3 us

profile of v8, /device:TPU:1, one launch (start us, length us, event | category | flops | bytes accessed | tf_op | source)
XLA Modules:
  0.0 30.9 jit_solution(16044245198339003969)
XLA Ops:
  0.6 27.2 %shard_map.41 = (f32[3,128]{1,0:T(4,128)S(1)}, f32[8,10,48,128]{3,2,1,0:T(8,128)S(1)}, f32[8,10,48,128]{3,2,1,0:T(8,128)S(1)}) custom-call(f32[8,8,32,128]{3,2,1,0:T(8,128)} %b_hbm.1, f32[8,32,128]{2,1,0:T(8,128)} %s_hbm.1), custom_call_target="tpu_custom_call" | custom-call | tf_op jit(solution)/shard_map/pallas_call | solution.py:449
  27.9 3.0 %shard_map.42 = (f32[8,8,32,128]{3,2,1,0:T(8,128)}, f32[1,8]{1,0:T(1,128)}) custom-call(f32[3,128]{1,0:T(4,128)S(1)} %get-tuple-element.7.gram_ref, f32[8,10,48,128]{3,2,1,0:T(8,128)S(1)} %get-tuple-element.8.buf_b, f32[8,10,48,128]{3,2,1,0:T(8,128)S(1)} %get-tuple-element.9.buf_a), custom_call_target="tpu_custom_call" | custom-call | tf_op jit(solution)/shard_map/pallas_call | solution.py:484

commit v9 on v8

--- a/solution.py
+++ b/solution.py
@@ -356,23 +356,23 @@
     row_two = as_row(gather(1, fourth, gather(0, third, blank)))
 
     late_done = spread(1, part_l, in_line, line, (row_two,))
+    for turn in both:
+        for way in both:
+            sent("x", way, [x_copy(turn, way, group) for group in range(GROUPS)])
+            sent("y", way, [y_copy(turn, way, part) for part in y_parts[turn]])
+            sent("z", way, [z_copy(turn, way, part) for part in both])
+    early_done.wait_send()
     early_done.wait_recv()
     early = added(part_e, len(line) + 1)
     late_done.wait_recv()
     late = added(part_l, len(line) + 1)
     chip = ix * chips_y + lax.div(row, 2)
     planes_done = spread(2, part_p, chip, plane, (early[0:1], early[1:2], late))
+    late_done.wait_send()
     planes_done.wait_recv()
     gram_ref[...] = added(part_p, len(plane) + 1)
 
-    early_done.wait_send()
-    late_done.wait_send()
     planes_done.wait_send()
-    for turn in both:
-        for way in both:
-            sent("x", way, [x_copy(turn, way, group) for group in range(GROUPS)])
-            sent("y", way, [y_copy(turn, way, part) for part in y_parts[turn]])
-            sent("z", way, [z_copy(turn, way, part) for part in both])
 
 
 def combine_kernel(gram_ref, buf_b, buf_a, x_hbm, norm_ref, buf_x, coeff, out_sem):

time: 31 us -> 30.9 us (level)
  no operation moved by 1% of the time
where the time goes in v9:
time: 30.9 us; the launch traced here: 30.8 us
  Pallas kernels  30.2 us (98%)
  between operations  0.64 us (2%)
    pallas_call x1, Pallas kernels, body(): pl.pallas_call(functools.partial(exchange_kernel, gx, gy, gz), out_shape=...  27.2 us
    pallas_call x1, Pallas kernels, body(): pl.pallas_call(combine_kernel, out_shape=(jax.ShapeDtypeStruct(block, f32...  3 us

profile of v9, /device:TPU:1, one launch (start us, length us, event | category | flops | bytes accessed | tf_op | source)
XLA Modules:
  0.0 30.8 jit_solution(9884377394671240905)
XLA Ops:
  0.6 27.2 %shard_map.41 = (f32[3,128]{1,0:T(4,128)S(1)}, f32[8,10,48,128]{3,2,1,0:T(8,128)S(1)}, f32[8,10,48,128]{3,2,1,0:T(8,128)S(1)}) custom-call(f32[8,8,32,128]{3,2,1,0:T(8,128)} %b_hbm.1, f32[8,32,128]{2,1,0:T(8,128)} %s_hbm.1), custom_call_target="tpu_custom_call" | custom-call | tf_op jit(solution)/shard_map/pallas_call | solution.py:449
  27.8 3.0 %shard_map.42 = (f32[8,8,32,128]{3,2,1,0:T(8,128)}, f32[1,8]{1,0:T(1,128)}) custom-call(f32[3,128]{1,0:T(4,128)S(1)} %get-tuple-element.7.gram_ref, f32[8,10,48,128]{3,2,1,0:T(8,128)S(1)} %get-tuple-element.8.buf_b, f32[8,10,48,128]{3,2,1,0:T(8,128)S(1)} %get-tuple-element.9.buf_a), custom_call_target="tpu_custom_call" | custom-call | tf_op jit(solution)/shard_map/pallas_call | solution.py:484

commit v10 on v8

--- a/solution.py
+++ b/solution.py
@@ -98,8 +98,7 @@
             device_id_type=MESH,
         )
 
-    spans = ((2, NX), (1, 2), (NX, NX + 1), (1, NX + 1))
-    y_parts = ((3,), (0, 1, 2))
+    spans = ((2, NX), (1, 2), (NX, NX + 1))
 
     def y_copy(turn, way, part):
         buf, (low, high) = bufs[turn], spans[part]
@@ -294,7 +293,7 @@
     tell(0, near)
     loads[2].wait()
     for way in both:
-        start("y", way, [y_copy(0, way, part) for part in y_parts[0]])
+        start("y", way, [y_copy(0, way, part) for part in range(3)])
     for part in both:
         pack_z(0, part)
     for way in both:
@@ -306,7 +305,7 @@
     row_zero = as_row(gather(0, zeroth, blank))
     pl.semaphore_wait(heard.at[0], len(near))
     tell(1, second)
-    take_y(buf_q, 0, y_parts[0])
+    take_y(buf_q, 0, range(3))
     for part in both:
         take_z(buf_q, 0, part)
 
@@ -371,7 +370,7 @@
     for turn in both:
         for way in both:
             sent("x", way, [x_copy(turn, way, group) for group in range(GROUPS)])
-            sent("y", way, [y_copy(turn, way, part) for part in y_parts[turn]])
+            sent("y", way, [y_copy(turn, way, part) for part in range(3)])
             sent("z", way, [z_copy(turn, way, part) for part in both])
 
 
@@ -469,8 +468,8 @@
                 dma((4,)),
                 dma((2, 2, GROUPS)),
                 dma((2, 2, GROUPS)),
-                dma((2, 2, 4)),
-                dma((2, 2, 4)),
+                dma((2, 2, 3)),
+                dma((2, 2, 3)),
                 dma((2, 2, 2)),
                 dma((2, 2, 2)),
                 dma((3,)),

time: 31 us -> 30.9 us (level)
  no operation moved by 1% of the time
where the time goes in v10:
time: 30.9 us; the launch traced here: 30.8 us
  Pallas kernels  30.2 us (98%)
  between operations  0.64 us (2%)
    pallas_call x1, Pallas kernels, body(): pl.pallas_call(functools.partial(exchange_kernel, gx, gy, gz), out_shape=...  27.2 us
    pallas_call x1, Pallas kernels, body(): pl.pallas_call(combine_kernel, out_shape=(jax.ShapeDtypeStruct(block, f32...  3 us

profile of v10, /device:TPU:1, one launch (start us, length us, event | category | flops | bytes accessed | tf_op | source)
XLA Modules:
  0.0 30.8 jit_solution(11980934790431106371)
XLA Ops:
  0.6 27.2 %shard_map.41 = (f32[3,128]{1,0:T(4,128)S(1)}, f32[8,10,48,128]{3,2,1,0:T(8,128)S(1)}, f32[8,10,48,128]{3,2,1,0:T(8,128)S(1)}) custom-call(f32[8,8,32,128]{3,2,1,0:T(8,128)} %b_hbm.1, f32[8,32,128]{2,1,0:T(8,128)} %s_hbm.1), custom_call_target="tpu_custom_call" | custom-call | tf_op jit(solution)/shard_map/pallas_call | solution.py:448
  27.8 3.0 %shard_map.42 = (f32[8,8,32,128]{3,2,1,0:T(8,128)}, f32[1,8]{1,0:T(1,128)}) custom-call(f32[3,128]{1,0:T(4,128)S(1)} %get-tuple-element.7.gram_ref, f32[8,10,48,128]{3,2,1,0:T(8,128)S(1)} %get-tuple-element.8.buf_b, f32[8,10,48,128]{3,2,1,0:T(8,128)S(1)} %get-tuple-element.9.buf_a), custom_call_target="tpu_custom_call" | custom-call | tf_op jit(solution)/shard_map/pallas_call | solution.py:483
